TPU v7x, 512 devices: a whole 4x8x8 slice. The times are simulated.
512 devices in a mesh: gx: 16 (over y, core), gy: 4 (over x), gz: 8 (over z).
Axes of the slice: x: 4, y: 8, z: 8, core: 2. Of those that a mesh axis runs over, the one named last changes fastest.
Arguments:
- fractions: float32 [3, 16, 8, 16, 128], P(None, 'gx', 'gy', 'gz'), may hold values from 0 to 1
- polarizability: float32 [16, 8, 16, 128], P('gx', 'gy', 'gz'), may hold values from 0.5 to 2
- occupancy: int32 [16, 8, 16, 128], P('gx', 'gy', 'gz'), may hold values 0 or 1
- pair_mask: int32 [16, 8, 16, 27], P('gx', 'gy', 'gz'), may hold values from 0 to 1, as said below
- perm_field: float32 [6, 16, 8, 16, 128], P(None, 'gx', 'gy', 'gz'), may hold values from -6 to 6
- history: float32 [6, 6, 16, 8, 16, 128], P(None, None, 'gx', 'gy', 'gz'), may hold values from -12 to 12
Outputs:
- induced: float32 [6, 16, 8, 16, 128], P(None, 'gx', 'gy', 'gz')
- change: float32 [], replicated
Inputs may be any that keep to these rules, and one draw needn't show every extreme that they name: pair_mask[t, k] equals pair_mask at tile t + offset(k) for the opposite offset 26 - k (periodic); pair_mask[t, 13] (the tile itself) is 1.
All inputs are finite; a program needn't handle non-finite values. No bound on the sum of `occupancy` on one device may be relied on, other than what follows from the above.
Results may differ from a plain program's by a relative error of at most 0.0003.
Values sent between devices are 32-bit elements; how exact they have to be, the bound alone decides.
A program may use at most 64 MiB of HBM per device.

v0:
```python
import functools

import jax
import jax.numpy as jnp
from jax import lax
from jax.experimental import pallas as pl
from jax.experimental.pallas import tpu as pltpu
from jax.sharding import PartitionSpec as P

CELL_EDGE = 10.0
SOFTENING = 0.3
THOLE_DAMP = 0.39
RELAXATION = 0.7
MESH = pl.DeviceIdType.MESH
AXES = ("gx", "gy", "gz")
ROWS = 8
BLOCK = 32
FIELD_BLOCK = 32


def halo_moves(devices, tiles):
    options = []
    for count, n in zip(devices, tiles):
        if count == 2 and n == 2:
            around = [(1, 0, 2, 2)]
        else:
            around = [(1, n - 1, 1, n + 1), (-1, 0, 1, n)]
        options.append([(0, 0, n, 0)] + around)
    return [
        (a, b, c) for a in options[0] for b in options[1] for c in options[2] if (a[0], b[0], c[0]) != (0, 0, 0)
    ]


def row_moves(devices, tiles, row):
    along_x, along_y, along_z = [
        [(0, 0, n, 0)] + [move[axis] for move in halo_moves(devices, tiles) if move[axis][0] != 0]
        for axis, n in enumerate(tiles)
    ]
    n = tiles[1]
    rows = [(0, row, 1, row)]
    if row == n - 1:
        rows.append((1, row, 1, n + 1))
    if row == 0:
        rows.append((-1, row, 1, n))
    along_x, along_z = list(dict.fromkeys(along_x)), list(dict.fromkeys(along_z))
    return [
        (a, b, c) for a in along_x for b in rows for c in along_z if (a[0], b[0], c[0]) != (0, 0, 0)
    ]


def solve_fit(total, past, lane, pair_lane):
    def pick(a, b):
        index = pair_lane[(min(a, b), max(a, b))]
        return jnp.sum(jnp.where(lane == index, total, 0.0), axis=1, keepdims=True)

    diagonal = [pick(a, a) for a in range(past)]
    trace = diagonal[0]
    for value in diagonal[1:]:
        trace = trace + value
    ridge = 0.001 * trace / past + 1.0
    lower, inverse = {}, []
    for j in range(past):
        pivot = diagonal[j] + ridge
        for m in range(j):
            pivot = pivot - lower[j, m] * lower[j, m]
        inverse.append(1.0 / jnp.sqrt(pivot))
        for i in range(j + 1, past):
            value = pick(i, j)
            for m in range(j):
                value = value - lower[i, m] * lower[j, m]
            lower[i, j] = value * inverse[j]
    forward = []
    for i in range(past):
        value = pick(i, past)
        for m in range(i):
            value = value - lower[i, m] * forward[m]
        forward.append(value * inverse[i])
    coeffs = [None] * past
    for i in reversed(range(past)):
        value = forward[i]
        for m in range(i + 1, past):
            value = value - lower[m, i] * coeffs[m]
        coeffs[i] = value * inverse[i]
    return coeffs


def kernel(
    devices,
    frac_in, pol_in, occ_in, mask_in, perm_in, hist_in,
    out_ref, change_ref,
    frac_ref, pol_ref, occ_ref, mask_ref, perm_ref, hist_ref,
    geom, held_one, held_two, past_sets, own, apart, pull, direct, sums, slots_a, slots_b,
    load_sem, send_all, recv_all, send_geom, recv_geom, send_one, recv_one, send_two, recv_two,
):
    tiles = tuple(frac_ref.shape[1:4])
    slots = frac_ref.shape[4]
    steps = hist_ref.shape[0]
    rows = hist_ref.shape[1]
    past = steps - 1
    total_devices = devices[0] * devices[1] * devices[2]
    at = [lax.axis_index(axis) for axis in AXES]
    me = (at[0] * devices[1] + at[1]) * devices[2] + at[2]
    moves = halo_moves(devices, tiles)
    lane = lax.broadcasted_iota(jnp.int32, (1, slots), 1)
    loads = [
        pltpu.make_async_copy(source, target, load_sem.at[number])
        for number, (source, target) in enumerate(
            (
                (hist_in, hist_ref), (occ_in, occ_ref), (frac_in, frac_ref),
                (pol_in, pol_ref), (perm_in, perm_ref), (mask_in, mask_ref),
            )
        )
    ]
    for load in loads:
        load.start()

    def each_other(act):
        def pair(step, carry):
            ahead = (step // devices[1], step % devices[1])
            first = []
            for axis in range(2):
                place = at[axis] + ahead[axis]
                first.append(jnp.where(place >= devices[axis], place - devices[axis], place))
            for shift in range(devices[2] - 1, -1, -1):
                last = at[2] + shift
                last = jnp.where(last >= devices[2], last - devices[2], last)
                if shift == 0:
                    @pl.when(step > 0)
                    def _():
                        act((first[0], first[1], last))
                else:
                    act((first[0], first[1], last))
            return carry

        lax.fori_loop(0, devices[0] * devices[1], pair, 0)

    barrier = pltpu.get_barrier_semaphore()

    each_other(
        lambda device: pl.semaphore_signal(barrier, inc=1, device_id=device, device_id_type=MESH)
    )
    for load in loads:
        load.wait()

    def everyone(index, held):
        def start(device):
            pltpu.make_async_remote_copy(
                src_ref=held.at[pl.ds(me, 1)],
                dst_ref=held.at[pl.ds(me, 1)],
                send_sem=send_all.at[index],
                recv_sem=recv_all.at[index],
                device_id=device,
                device_id_type=MESH,
            ).start()

        each_other(start)

    def everyone_wait(index, held):
        whole = pltpu.make_async_remote_copy(
            src_ref=held.at[pl.ds(0, total_devices - 1)],
            dst_ref=held.at[pl.ds(0, total_devices - 1)],
            send_sem=send_all.at[index],
            recv_sem=recv_all.at[index],
            device_id=(at[0], at[1], (at[2] + 1) % devices[2]),
            device_id_type=MESH,
        )
        whole.wait_send()
        whole.wait_recv()

    def halo(held, send, recv, moves=moves):
        copies = []
        for number, move in enumerate(moves):
            source = tuple(pl.ds(part[1], part[2]) for part in move)
            place = tuple(pl.ds(part[3], part[2]) for part in move)
            target = tuple((at[axis] + move[axis][0] + devices[axis]) % devices[axis] for axis in range(3))
            copies.append(
                pltpu.make_async_remote_copy(
                    src_ref=held.at[source],
                    dst_ref=held.at[place],
                    send_sem=send.at[number],
                    recv_sem=recv.at[number],
                    device_id=target,
                    device_id_type=MESH,
                )
            )
        return copies

    places = [(x, y, z) for x in range(tiles[0]) for y in range(tiles[1]) for z in range(tiles[2])]
    zero_row = jnp.zeros((1, slots), jnp.float32)
    spare = jnp.zeros((ROWS - rows, slots), jnp.float32)
    filled, scaled, fixed = [], [], []
    for t, (x, y, z) in enumerate(places):
        full = occ_ref[x, y, z, :].reshape(1, slots).astype(jnp.float32)
        pol = pol_ref[x, y, z, :].reshape(1, slots)
        scaled.append(RELAXATION * full * pol)
        tile = jnp.concatenate(
            [frac_ref[c, x, y, z, :].reshape(1, slots) * CELL_EDGE for c in range(3)]
            + [lax.rsqrt(pol)] + [zero_row] * (ROWS - 4),
            axis=0,
        )
        geom[x, y, z] = tile
        for h in range(steps):
            moment = jnp.concatenate(
                [hist_ref[h, c, x, y, z, :].reshape(1, slots) for c in range(rows)], axis=0
            )
            past_sets[h, t] = jnp.concatenate([moment * full, spare], axis=0)
        fixed.append(
            jnp.concatenate(
                [perm_ref[c, x, y, z, :].reshape(1, slots) for c in range(rows)] + [spare], axis=0
            )
        )
    pair_lane = {}
    gram = zero_row
    for a in range(steps):
        for b in range(a, steps):
            product = past_sets[a, 0] * past_sets[b, 0]
            for t in range(1, len(places)):
                product = product + past_sets[a, t] * past_sets[b, t]
            value = jnp.sum(jnp.sum(product, axis=0, keepdims=True), axis=1, keepdims=True)
            pair_lane[(a, b)] = len(pair_lane)
            gram = jnp.where(lane == pair_lane[(a, b)], value, gram)
    slots_a[pl.ds(me, 1)] = gram.reshape(1, 1, slots)

    for t, (x, y, z) in enumerate(places):
        for c in range(4):
            row = geom[x, y, z, c, :].reshape(1, slots)
            own[t, c] = jnp.broadcast_to(row, (slots, slots)).T

    pl.semaphore_wait(barrier, total_devices - 1)
    geom_copies = halo(geom, send_geom, recv_geom)
    everyone(0, slots_a)
    for copy in geom_copies:
        copy.start()

    def clear(step, carry):
        sums[step] = jnp.zeros((rows, slots, slots), jnp.float32)
        return carry

    lax.fori_loop(0, 2 * len(places), clear, 0)
    for move, copy in zip(moves, geom_copies):
        if move[0][0] == 0:
            copy.wait()

    wraps = tuple(n + 2 for n in tiles)

    def wrap(value, size):
        return jnp.where(value < 0, value + size, value)

    def spot(t):
        x = t // (tiles[1] * tiles[2])
        y = t // tiles[2] % tiles[1]
        z = t % tiles[2]
        return (x, y, z)

    def source_rows(held, place, names):
        return [held[place[0], place[1], place[2], pl.ds(c, 1), :] for c in names]

    def geometry(t, nine):
        along_x, along_y = nine // 3 - 1, nine % 3 - 1
        base = spot(t)
        for along_z in (-1, 0, 1):
            along = (along_x, along_y, along_z)
            k = nine * 3 + along_z + 1
            place = tuple(wrap(base[i] + along[i], wraps[i]) for i in range(3))
            source = source_rows(geom, place, range(4))
            source[0] = source[0] + CELL_EDGE * along_x.astype(jnp.float32)
            source[1] = source[1] + CELL_EDGE * along_y.astype(jnp.float32)
            source[2] = source[2] + CELL_EDGE * along_z
            damp = source[3] * THOLE_DAMP
            allowed = mask_ref[base[0], base[1], base[2], k].astype(jnp.float32)
            for first in range(0, slots, BLOCK):
                part = pl.ds(first, BLOCK)
                dx = source[0] - own[t, 0, part, :]
                dy = source[1] - own[t, 1, part, :]
                dz = source[2] - own[t, 2, part, :]
                square = dx * dx + dy * dy + dz * dz + SOFTENING
                root = lax.rsqrt(square)
                root_two = root * root
                cube = root_two * root * allowed
                arg = (square * square) * root * (damp * own[t, 3, part, :])
                fade = jnp.exp(-arg)
                three = 1.0 - fade
                five = three - arg * fade
                direct[t, k, part, :] = three * cube
                radial = five * cube * (3.0 * root_two)
                for i, d in enumerate((dx, dy, dz)):
                    apart[i, t, k, part, :] = d
                    pull[i, t, k, part, :] = radial * d

    count = len(places)

    def same_x(step, carry):
        geometry(step // 3, 3 + step % 3)
        return carry

    def other_x(step, carry):
        part = step % 6
        geometry(step // 6, jnp.where(part < 3, part, part + 3))
        return carry

    lax.fori_loop(0, count * 3, same_x, 0)

    everyone_wait(0, slots_a)
    total = jnp.sum(slots_a[...], axis=0)
    coeffs = solve_fit(total, past, lane, pair_lane)
    for t, (x, y, z) in enumerate(places):
        value = coeffs[0] * past_sets[1, t]
        for h in range(1, past):
            value = value + coeffs[h] * past_sets[h + 1, t]
        held_one[x, y, z] = value
    one_copies = halo(held_one, send_one, recv_one)
    for copy in one_copies:
        copy.start()
    for move, copy in zip(moves, geom_copies):
        if move[0][0] != 0:
            copy.wait()
    lax.fori_loop(0, count * 6, other_x, 0)
    off_diagonal = lax.broadcasted_iota(jnp.int32, (slots, slots), 0) != lax.broadcasted_iota(
        jnp.int32, (slots, slots), 1
    )
    for t in range(count):
        direct[t, 13] = jnp.where(off_diagonal, direct[t, 13], 0.0)

    blocks = slots // FIELD_BLOCK

    def add_sources(held, index, step, base, along_y):
        part = pl.ds(pl.multiple_of(step % blocks * FIELD_BLOCK, FIELD_BLOCK), FIELD_BLOCK)
        t = (base[0] * tiles[1] + base[1]) * tiles[2] + base[2]
        place_y = wrap(base[1] + along_y, wraps[1])

        def plane(along_x, acc):
            acc = list(acc)
            place_x = wrap(base[0] + along_x, wraps[0])
            for along_z in (-1, 0, 1):
                place = (place_x, place_y, wrap(base[2] + along_z, wraps[2]))
                moment = source_rows(held, place, range(rows))
                k = 9 * (along_x + 1) + 3 * (along_y + 1) + along_z + 1
                d = direct[t, k, part, :]
                away = [apart[i, t, k, part, :] for i in range(3)]
                drawn = [pull[i, t, k, part, :] for i in range(3)]
                for s in range(rows // 3):
                    m = moment[3 * s : 3 * s + 3]
                    project = away[0] * m[0] + away[1] * m[1] + away[2] * m[2]
                    for i in range(3):
                        acc[3 * s + i] = acc[3 * s + i] + (project * drawn[i] - d * m[i])
            return tuple(acc)

        acc = lax.fori_loop(
            -1, 2, plane, tuple(sums[index * count + t, c, part, :] for c in range(rows))
        )
        for c in range(rows):
            sums[index * count + t, c, part, :] = acc[c]

    flat = tiles[0] * tiles[2] * blocks

    def to_row(held, index, row):
        def one(step, carry):
            column = step // blocks % (tiles[0] * tiles[2])
            base = (column // tiles[2], row, column % tiles[2])
            add_sources(held, index, step, base, step // flat - 1)
            return carry

        lax.fori_loop(0, 3 * flat, one, 0)

    def from_row(held, index, row):
        def one(step, carry):
            column = step // blocks % (tiles[0] * tiles[2])
            along_y = step // flat - 1
            base = (column // tiles[2], (row - along_y + tiles[1]) % tiles[1], column % tiles[2])
            add_sources(held, index, step, base, along_y)
            return carry

        lax.fori_loop(0, 3 * flat, one, 0)

    square_lane = lax.broadcasted_iota(jnp.int32, (slots, slots), 1)

    def field_of(index, t):
        columns = jnp.zeros((slots, slots), jnp.float32)
        for c in range(rows):
            value = jnp.sum(sums[index * count + t, c], axis=1, keepdims=True)
            columns = jnp.where(square_lane == c, value, columns)
        return columns.T[0:ROWS]

    for copy in one_copies:
        copy.wait()
    two_copies = []
    for row in range(tiles[1]):
        to_row(held_one, 0, row)
        for t, (x, y, z) in enumerate(places):
            if y == row:
                held_two[x, y, z] = (1.0 - RELAXATION) * held_one[x, y, z] + scaled[t] * (
                    fixed[t] + field_of(0, t)
                )
        copies = halo(held_two, send_two.at[row], recv_two.at[row], row_moves(devices, tiles, row))
        for copy in copies:
            copy.start()
        two_copies.append(copies)
    for row in range(tiles[1]):
        for copy in two_copies[row]:
            copy.wait()
        from_row(held_two, 1, row)
    fields = [field_of(1, t) for t in range(count)]
    changed = jnp.zeros((ROWS, slots), jnp.float32)
    size = jnp.zeros((ROWS, slots), jnp.float32)
    for t, (x, y, z) in enumerate(places):
        before = held_two[x, y, z]
        after = (1.0 - RELAXATION) * before + scaled[t] * (fixed[t] + fields[t])
        for c in range(rows):
            out_ref[c, x, y, z, :] = after[c]
        changed = changed + (after - before) * (after - before)
        size = size + after * after

    def all_of(value):
        return jnp.sum(jnp.sum(value, axis=0, keepdims=True), axis=1, keepdims=True)

    pair = jnp.where(lane == 0, all_of(changed), jnp.where(lane == 1, all_of(size), 0.0))
    slots_b[pl.ds(me, 1)] = pair.reshape(1, 1, slots)
    everyone(1, slots_b)
    everyone_wait(1, slots_b)
    pair = jnp.sum(slots_b[...], axis=0)
    above = jnp.sum(jnp.where(lane == 0, pair, 0.0), axis=1, keepdims=True)
    below = jnp.sum(jnp.where(lane == 1, pair, 0.0), axis=1, keepdims=True)
    change_ref[...] = jnp.broadcast_to(jnp.sqrt(above / (below + 1.0)), (1, slots))


def solution(mesh):
    devices = tuple(mesh.shape[axis] for axis in AXES)
    total_devices = devices[0] * devices[1] * devices[2]

    def on_device(fractions, polarizability, occupancy, pair_mask, perm_field, history):
        tiles = fractions.shape[1:4]
        slots = fractions.shape[4]
        count = tiles[0] * tiles[1] * tiles[2]
        wraps = tuple(n + 2 for n in tiles)
        moves = len(halo_moves(devices, tiles))
        rows = history.shape[1]
        vmem = pl.BlockSpec(memory_space=pltpu.VMEM)
        f32 = jnp.float32
        induced, change = pl.pallas_call(
            functools.partial(kernel, devices),
            out_shape=(
                jax.ShapeDtypeStruct(perm_field.shape, f32),
                jax.ShapeDtypeStruct((1, slots), f32),
            ),
            in_specs=[pl.BlockSpec(memory_space=pltpu.HBM)] * 6,
            out_specs=(vmem, vmem),
            scratch_shapes=[
                pltpu.VMEM(fractions.shape, f32),
                pltpu.VMEM(polarizability.shape, f32),
                pltpu.VMEM(occupancy.shape, jnp.int32),
                pltpu.SMEM(pair_mask.shape, jnp.int32),
                pltpu.VMEM(perm_field.shape, f32),
                pltpu.VMEM(history.shape, f32),
                pltpu.VMEM(wraps + (ROWS, slots), f32),
                pltpu.VMEM(wraps + (ROWS, slots), f32),
                pltpu.VMEM(wraps + (ROWS, slots), f32),
                pltpu.VMEM((history.shape[0], count, ROWS, slots), f32),
                pltpu.VMEM((count, 4, slots, slots), f32),
                pltpu.VMEM((3, count, 27, slots, slots), f32),
                pltpu.VMEM((3, count, 27, slots, slots), f32),
                pltpu.VMEM((count, 27, slots, slots), f32),
                pltpu.VMEM((2 * count, rows, slots, slots), f32),
                pltpu.VMEM((total_devices, 1, slots), f32),
                pltpu.VMEM((total_devices, 1, slots), f32),
                pltpu.SemaphoreType.DMA((6,)),
                pltpu.SemaphoreType.DMA((2,)),
                pltpu.SemaphoreType.DMA((2,)),
            ]
            + [pltpu.SemaphoreType.DMA((moves,))] * 4
            + [pltpu.SemaphoreType.DMA((tiles[1], moves))] * 2,
            compiler_params=pltpu.CompilerParams(
                collective_id=0, has_side_effects=True, vmem_limit_bytes=67043328
            ),
        )(fractions, polarizability, occupancy, pair_mask, perm_field, history)
        return induced, change[0, 0]

    in_specs = (
        P(None, "gx", "gy", "gz", None),
        P("gx", "gy", "gz", None),
        P("gx", "gy", "gz", None),
        P("gx", "gy", "gz", None),
        P(None, "gx", "gy", "gz", None),
        P(None, None, "gx", "gy", "gz", None),
    )
    out_specs = (P(None, "gx", "gy", "gz", None), P())
    return jax.shard_map(
        on_device, mesh=mesh, in_specs=in_specs, out_specs=out_specs, check_vma=False
    )
```

profile of v0, /device:TPU:1, one launch (start us, length us, event | category | flops | bytes accessed | tf_op | source)
XLA Modules:
  0.0 85.7 jit_solution(14469216562826782626)
XLA Ops:
  0.6 82.6 %shard_map.77 = (f32[6,1,2,2,128]{4,3,2,1,0:T(2,128)}, f32[1,128]{1,0:T(1,128)}) custom-call(f32[3,1,2,2,128]{4,3,2,1,0:T(2,128)} %frac_in.1, f32[1,2,2,128]{3,2,1,0:T(2,128)} %pol_in.1, s32[1,2,2,128]{3,2,1,0:T(2,128)} %occ_in.1, s32[1,2,2,27]{3,2,1,0:T(2,128)} %mask_in.1, f32[6,1,2,2,128]{4,3,2,1,0:T(2,128)} %perm_in.1, f32[6,6,1,2,2,128]{5,4,3,2,1,0:T(2,128)} %hist_in.1), custom_call_target="tpu_custom_call" | custom-call | tf_op jit(solution)/shard_map/pallas_call | solution.py:439
  83.2 0.0 copy-start
  83.2 1.3 %copy.10 = f32[6,1,2,2,128]{4,3,2,1,0:T(2,128)} copy(f32[6,1,2,2,128]{4,3,2,1,0:T(2,128)} %get-tuple-element.8) | data formatting | bytes 24576
  84.5 0.0 copy-done
Async XLA Ops:
  83.2 1.3 %copy-start = (f32[1,128]{1,0:T(1,128)S(1)}, f32[1,128]{1,0:T(1,128)}, u32[]{:S(2)}) copy-start(f32[1,128]{1,0:T(1,128)} %get-tuple-element.5) | copy-start | bytes 1540
where the time goes:
time: 85.9 us; the launch traced here: 85.7 us
  Pallas kernels  82.6 us (96%)
  between operations  1.81 us (2%)
  local copies, waits for them, and re-layouts  1.31 us (2%)
    pallas_call x1, Pallas kernels, on_device(): pl.pallas_call(functools.partial(kernel, devices), out_shape=(jax.ShapeDt...  82.6 us

commit v1 on v0

--- a/solution.py
+++ b/solution.py
@@ -89,7 +89,7 @@
     frac_in, pol_in, occ_in, mask_in, perm_in, hist_in,
     out_ref, change_ref,
     frac_ref, pol_ref, occ_ref, mask_ref, perm_ref, hist_ref,
-    geom, held_one, held_two, past_sets, own, apart, pull, direct, sums, slots_a, slots_b,
+    geom, held_one, held_two, past_sets, own, apart, pull, direct, sums, slots_a, slots_b, slots_c, slots_d,
     load_sem, send_all, recv_all, send_geom, recv_geom, send_one, recv_one, send_two, recv_two,
 ):
     tiles = tuple(frac_ref.shape[1:4])
@@ -97,9 +97,7 @@
     steps = hist_ref.shape[0]
     rows = hist_ref.shape[1]
     past = steps - 1
-    total_devices = devices[0] * devices[1] * devices[2]
     at = [lax.axis_index(axis) for axis in AXES]
-    me = (at[0] * devices[1] + at[1]) * devices[2] + at[2]
     moves = halo_moves(devices, tiles)
     lane = lax.broadcasted_iota(jnp.int32, (1, slots), 1)
     loads = [
@@ -114,58 +112,72 @@
     for load in loads:
         load.start()
 
-    def each_other(act):
-        def pair(step, carry):
-            ahead = (step // devices[1], step % devices[1])
-            first = []
-            for axis in range(2):
-                place = at[axis] + ahead[axis]
-                first.append(jnp.where(place >= devices[axis], place - devices[axis], place))
-            for shift in range(devices[2] - 1, -1, -1):
-                last = at[2] + shift
-                last = jnp.where(last >= devices[2], last - devices[2], last)
-                if shift == 0:
-                    @pl.when(step > 0)
-                    def _():
-                        act((first[0], first[1], last))
-                else:
-                    act((first[0], first[1], last))
-            return carry
-
-        lax.fori_loop(0, devices[0] * devices[1], pair, 0)
+    groups = ((0,), (1, 2))
+
+    def size_of(axes):
+        total = 1
+        for axis in axes:
+            total *= devices[axis]
+        return total
+
+    def shifted(shift):
+        places = []
+        for axis in range(3):
+            place = at[axis] + shift[axis]
+            places.append(jnp.where(place >= devices[axis], place - devices[axis], place))
+        return tuple(places)
+
+    def hops(shift):
+        return sum(min(part, n - part) for part, n in zip(shift, devices))
+
+    def shifts_of(axes):
+        spans = [range(devices[axis]) if axis in axes else range(1) for axis in range(3)]
+        every = [(x, y, z) for x in spans[0] for y in spans[1] for z in spans[2] if (x, y, z) != (0, 0, 0)]
+        return sorted(every, key=lambda shift: -hops(shift))
+
+    def rank_in(axes):
+        rank = 0
+        for axis in axes:
+            rank = rank * devices[axis] + at[axis]
+        return rank
+
+    near = [tuple((move[axis][0] + devices[axis]) % devices[axis] for axis in range(3)) for move in moves]
+    greeted = list(dict.fromkeys([shift for axes in groups for shift in shifts_of(axes)] + near))
 
     barrier = pltpu.get_barrier_semaphore()
 
-    each_other(
-        lambda device: pl.semaphore_signal(barrier, inc=1, device_id=device, device_id_type=MESH)
-    )
+    for shift in greeted:
+        pl.semaphore_signal(barrier, inc=1, device_id=shifted(shift), device_id_type=MESH)
     for load in loads:
         load.wait()
 
-    def everyone(index, held):
-        def start(device):
+    def share(index, stage, held, value):
+        axes = groups[stage]
+        rank = rank_in(axes)
+        held[pl.ds(rank, 1)] = value.reshape(1, 1, slots)
+        for shift in shifts_of(axes):
             pltpu.make_async_remote_copy(
-                src_ref=held.at[pl.ds(me, 1)],
-                dst_ref=held.at[pl.ds(me, 1)],
-                send_sem=send_all.at[index],
-                recv_sem=recv_all.at[index],
-                device_id=device,
+                src_ref=held.at[pl.ds(rank, 1)],
+                dst_ref=held.at[pl.ds(rank, 1)],
+                send_sem=send_all.at[index, stage],
+                recv_sem=recv_all.at[index, stage],
+                device_id=shifted(shift),
                 device_id_type=MESH,
             ).start()
 
-        each_other(start)
-
-    def everyone_wait(index, held):
+    def collect(index, stage, held):
+        others = size_of(groups[stage]) - 1
         whole = pltpu.make_async_remote_copy(
-            src_ref=held.at[pl.ds(0, total_devices - 1)],
-            dst_ref=held.at[pl.ds(0, total_devices - 1)],
-            send_sem=send_all.at[index],
-            recv_sem=recv_all.at[index],
-            device_id=(at[0], at[1], (at[2] + 1) % devices[2]),
+            src_ref=held.at[pl.ds(0, others)],
+            dst_ref=held.at[pl.ds(0, others)],
+            send_sem=send_all.at[index, stage],
+            recv_sem=recv_all.at[index, stage],
+            device_id=shifted((0, 0, 1)),
             device_id_type=MESH,
         )
         whole.wait_send()
         whole.wait_recv()
+        return jnp.sum(held[...], axis=0)
 
     def halo(held, send, recv, moves=moves):
         copies = []
@@ -219,16 +231,15 @@
             value = jnp.sum(jnp.sum(product, axis=0, keepdims=True), axis=1, keepdims=True)
             pair_lane[(a, b)] = len(pair_lane)
             gram = jnp.where(lane == pair_lane[(a, b)], value, gram)
-    slots_a[pl.ds(me, 1)] = gram.reshape(1, 1, slots)
 
     for t, (x, y, z) in enumerate(places):
         for c in range(4):
             row = geom[x, y, z, c, :].reshape(1, slots)
             own[t, c] = jnp.broadcast_to(row, (slots, slots)).T
 
-    pl.semaphore_wait(barrier, total_devices - 1)
+    pl.semaphore_wait(barrier, len(greeted))
     geom_copies = halo(geom, send_geom, recv_geom)
-    everyone(0, slots_a)
+    share(0, 0, slots_a, gram)
     for copy in geom_copies:
         copy.start()
 
@@ -298,10 +309,10 @@
         geometry(step // 6, jnp.where(part < 3, part, part + 3))
         return carry
 
-    lax.fori_loop(0, count * 3, same_x, 0)
-
-    everyone_wait(0, slots_a)
-    total = jnp.sum(slots_a[...], axis=0)
+    lax.fori_loop(0, count * 2, same_x, 0)
+    share(0, 1, slots_b, collect(0, 0, slots_a))
+    lax.fori_loop(count * 2, count * 3, same_x, 0)
+    total = collect(0, 1, slots_b)
     coeffs = solve_fit(total, past, lane, pair_lane)
     for t, (x, y, z) in enumerate(places):
         value = coeffs[0] * past_sets[1, t]
@@ -414,10 +425,9 @@
         return jnp.sum(jnp.sum(value, axis=0, keepdims=True), axis=1, keepdims=True)
 
     pair = jnp.where(lane == 0, all_of(changed), jnp.where(lane == 1, all_of(size), 0.0))
-    slots_b[pl.ds(me, 1)] = pair.reshape(1, 1, slots)
-    everyone(1, slots_b)
-    everyone_wait(1, slots_b)
-    pair = jnp.sum(slots_b[...], axis=0)
+    share(1, 0, slots_c, pair)
+    share(1, 1, slots_d, collect(1, 0, slots_c))
+    pair = collect(1, 1, slots_d)
     above = jnp.sum(jnp.where(lane == 0, pair, 0.0), axis=1, keepdims=True)
     below = jnp.sum(jnp.where(lane == 1, pair, 0.0), axis=1, keepdims=True)
     change_ref[...] = jnp.broadcast_to(jnp.sqrt(above / (below + 1.0)), (1, slots))
@@ -425,7 +435,6 @@
 
 def solution(mesh):
     devices = tuple(mesh.shape[axis] for axis in AXES)
-    total_devices = devices[0] * devices[1] * devices[2]
 
     def on_device(fractions, polarizability, occupancy, pair_mask, perm_field, history):
         tiles = fractions.shape[1:4]
@@ -460,11 +469,13 @@
                 pltpu.VMEM((3, count, 27, slots, slots), f32),
                 pltpu.VMEM((count, 27, slots, slots), f32),
                 pltpu.VMEM((2 * count, rows, slots, slots), f32),
-                pltpu.VMEM((total_devices, 1, slots), f32),
-                pltpu.VMEM((total_devices, 1, slots), f32),
+                pltpu.VMEM((devices[0], 1, slots), f32),
+                pltpu.VMEM((devices[1] * devices[2], 1, slots), f32),
+                pltpu.VMEM((devices[0], 1, slots), f32),
+                pltpu.VMEM((devices[1] * devices[2], 1, slots), f32),
                 pltpu.SemaphoreType.DMA((6,)),
-                pltpu.SemaphoreType.DMA((2,)),
-                pltpu.SemaphoreType.DMA((2,)),
+                pltpu.SemaphoreType.DMA((2, 2)),
+                pltpu.SemaphoreType.DMA((2, 2)),
             ]
             + [pltpu.SemaphoreType.DMA((moves,))] * 4
             + [pltpu.SemaphoreType.DMA((tiles[1], moves))] * 2,

time: 85.9 us -> 73 us (0.85)
  Pallas kernels: 82.6 us -> 69.7 us
    pallas_call x1, Pallas kernels: 82.6 us -> 69.7 us  [on_device(): pl.pallas_call(functools.partial(kernel, devices), out_shape=(jax.ShapeDt...]
where the time goes in v1:
time: 73 us; the launch traced here: 72.8 us
  Pallas kernels  69.7 us (95%)
  between operations  1.81 us (2%)
  local copies, waits for them, and re-layouts  1.31 us (2%)
    pallas_call x1, Pallas kernels, on_device(): pl.pallas_call(functools.partial(kernel, devices), out_shape=(jax.ShapeDt...  69.7 us

profile of v1, /device:TPU:1, one launch (start us, length us, event | category | flops | bytes accessed | tf_op | source)
XLA Modules:
  0.0 72.8 jit_solution(7218551181737227473)
XLA Ops:
  0.6 69.7 %shard_map.77 = (f32[6,1,2,2,128]{4,3,2,1,0:T(2,128)}, f32[1,128]{1,0:T(1,128)}) custom-call(f32[3,1,2,2,128]{4,3,2,1,0:T(2,128)} %frac_in.1, f32[1,2,2,128]{3,2,1,0:T(2,128)} %pol_in.1, s32[1,2,2,128]{3,2,1,0:T(2,128)} %occ_in.1, s32[1,2,2,27]{3,2,1,0:T(2,128)} %mask_in.1, f32[6,1,2,2,128]{4,3,2,1,0:T(2,128)} %perm_in.1, f32[6,6,1,2,2,128]{5,4,3,2,1,0:T(2,128)} %hist_in.1), custom_call_target="tpu_custom_call" | custom-call | tf_op jit(solution)/shard_map/pallas_call | solution.py:448
  70.3 0.0 copy-start
  70.3 1.3 %copy.10 = f32[6,1,2,2,128]{4,3,2,1,0:T(2,128)} copy(f32[6,1,2,2,128]{4,3,2,1,0:T(2,128)} %get-tuple-element.8) | data formatting | bytes 24576
  71.6 0.0 copy-done
Async XLA Ops:
  70.3 1.3 %copy-start = (f32[1,128]{1,0:T(1,128)S(1)}, f32[1,128]{1,0:T(1,128)}, u32[]{:S(2)}) copy-start(f32[1,128]{1,0:T(1,128)} %get-tuple-element.5) | copy-start | bytes 1540

commit v2 on v1

v2 whole, which is shorter than its diff:
```python
import functools

import jax
import jax.numpy as jnp
from jax import lax
from jax.experimental import pallas as pl
from jax.experimental.pallas import tpu as pltpu
from jax.sharding import PartitionSpec as P

CELL_EDGE = 10.0
SOFTENING = 0.3
THOLE_DAMP = 0.39
RELAXATION = 0.7
LOG2E = 1.4426950408889634
MESH = pl.DeviceIdType.MESH
AXES = ("gx", "gy", "gz")
ROWS = 8
BLOCK = 32
GROUPS = ((0,), (1, 2))


def halo_moves(tiles):
    options = []
    for n in tiles:
        options.append([(0, 0, n, 0), (1, n - 1, 1, n + 1), (-1, 0, 1, n)])
    return [
        (a, b, c) for a in options[0] for b in options[1] for c in options[2] if (a[0], b[0], c[0]) != (0, 0, 0)
    ]


def solve_fit(total, past, lane, pair_lane):
    def pick(a, b):
        index = pair_lane[(min(a, b), max(a, b))]
        return jnp.sum(jnp.where(lane == index, total, 0.0), axis=1, keepdims=True)

    diagonal = [pick(a, a) for a in range(past)]
    trace = diagonal[0]
    for value in diagonal[1:]:
        trace = trace + value
    ridge = 0.001 * trace / past + 1.0
    lower, inverse = {}, []
    for j in range(past):
        pivot = diagonal[j] + ridge
        for m in range(j):
            pivot = pivot - lower[j, m] * lower[j, m]
        inverse.append(lax.rsqrt(pivot))
        for i in range(j + 1, past):
            value = pick(i, j)
            for m in range(j):
                value = value - lower[i, m] * lower[j, m]
            lower[i, j] = value * inverse[j]
    forward = []
    for i in range(past):
        value = pick(i, past)
        for m in range(i):
            value = value - lower[i, m] * forward[m]
        forward.append(value * inverse[i])
    coeffs = [None] * past
    for i in reversed(range(past)):
        value = forward[i]
        for m in range(i + 1, past):
            value = value - lower[m, i] * coeffs[m]
        coeffs[i] = value * inverse[i]
    return coeffs


def kernel(
    devices,
    frac_in, pol_in, occ_in, mask_in, perm_in, hist_in,
    out_ref, change_ref,
    frac_ref, pol_ref, occ_ref, mask_ref, perm_ref, hist_ref,
    geom, held_past, held_two, past_sets, spots, columns, features, weights,
    slots_a, slots_b, slots_c, slots_d,
    load_sem, send_all, recv_all, send_geom, recv_geom, send_past, recv_past, send_two, recv_two,
):
    tiles = tuple(frac_ref.shape[1:4])
    wraps = tuple(n + 2 for n in tiles)
    slots = frac_ref.shape[4]
    steps = hist_ref.shape[0]
    rows = hist_ref.shape[1]
    past = steps - 1
    at = [lax.axis_index(axis) for axis in AXES]
    moves = halo_moves(tiles)
    lane = lax.broadcasted_iota(jnp.int32, (1, slots), 1)
    loads = [
        pltpu.make_async_copy(source, target, load_sem.at[number])
        for number, (source, target) in enumerate(
            (
                (hist_in, hist_ref), (occ_in, occ_ref), (frac_in, frac_ref),
                (pol_in, pol_ref), (perm_in, perm_ref), (mask_in, mask_ref),
            )
        )
    ]
    for load in loads:
        load.start()

    def size_of(axes):
        total = 1
        for axis in axes:
            total *= devices[axis]
        return total

    def shifted(shift):
        places = []
        for axis in range(3):
            place = at[axis] + shift[axis]
            places.append(jnp.where(place >= devices[axis], place - devices[axis], place))
        return tuple(places)

    def hops(shift):
        return sum(min(part, n - part) for part, n in zip(shift, devices))

    def shifts_of(axes):
        spans = [range(devices[axis]) if axis in axes else range(1) for axis in range(3)]
        every = [(x, y, z) for x in spans[0] for y in spans[1] for z in spans[2] if (x, y, z) != (0, 0, 0)]
        return sorted(every, key=lambda shift: -hops(shift))

    def rank_in(axes):
        rank = 0
        for axis in axes:
            rank = rank * devices[axis] + at[axis]
        return rank

    near = [tuple((move[axis][0] + devices[axis]) % devices[axis] for axis in range(3)) for move in moves]
    greeted = list(dict.fromkeys([shift for axes in GROUPS for shift in shifts_of(axes)] + near))

    barrier = pltpu.get_barrier_semaphore()

    for shift in greeted:
        pl.semaphore_signal(barrier, inc=1, device_id=shifted(shift), device_id_type=MESH)
    for load in loads:
        load.wait()

    def share(index, stage, held, value):
        axes = GROUPS[stage]
        rank = rank_in(axes)
        held[pl.ds(rank, 1)] = value.reshape(1, 1, slots)
        for shift in shifts_of(axes):
            pltpu.make_async_remote_copy(
                src_ref=held.at[pl.ds(rank, 1)],
                dst_ref=held.at[pl.ds(rank, 1)],
                send_sem=send_all.at[index, stage],
                recv_sem=recv_all.at[index, stage],
                device_id=shifted(shift),
                device_id_type=MESH,
            ).start()

    def collect(index, stage, held):
        others = size_of(GROUPS[stage]) - 1
        whole = pltpu.make_async_remote_copy(
            src_ref=held.at[pl.ds(0, others)],
            dst_ref=held.at[pl.ds(0, others)],
            send_sem=send_all.at[index, stage],
            recv_sem=recv_all.at[index, stage],
            device_id=shifted((0, 0, 1)),
            device_id_type=MESH,
        )
        whole.wait_send()
        whole.wait_recv()
        return jnp.sum(held[...], axis=0)

    def halo(held, send, recv):
        copies = []
        for number, move in enumerate(moves):
            source = tuple(pl.ds(part[1], part[2]) for part in move)
            place = tuple(pl.ds(part[3], part[2]) for part in move)
            copies.append(
                pltpu.make_async_remote_copy(
                    src_ref=held.at[source],
                    dst_ref=held.at[place],
                    send_sem=send.at[number],
                    recv_sem=recv.at[number],
                    device_id=shifted(near[number]),
                    device_id_type=MESH,
                )
            )
        return copies

    def row_of(c):
        return 2 * (c % 3) + c // 3

    order = sorted(range(rows), key=row_of)
    places = [(x, y, z) for x in range(tiles[0]) for y in range(tiles[1]) for z in range(tiles[2])]
    count = len(places)
    zero_row = jnp.zeros((1, slots), jnp.float32)
    spare = jnp.zeros((ROWS - rows, slots), jnp.float32)
    scaled = []
    for t, (x, y, z) in enumerate(places):
        full = occ_ref[x, y, z, :].reshape(1, slots).astype(jnp.float32)
        pol = pol_ref[x, y, z, :].reshape(1, slots)
        scaled.append(RELAXATION * full * pol)
        parts = []
        for c in range(3):
            parts += [frac_ref[c, x, y, z, :].reshape(1, slots) * CELL_EDGE] * 2
        geom[x, y, z] = jnp.concatenate(parts + [lax.rsqrt(pol), zero_row], axis=0)
        for h in range(steps):
            moment = jnp.concatenate(
                [hist_ref[h, c, x, y, z, :].reshape(1, slots) for c in order] + [spare], axis=0
            ) * full
            past_sets[h, t] = moment
            if h > 0:
                held_past[x, y, z, pl.ds(ROWS * (h - 1), ROWS), :] = moment
    pair_lane = {}
    gram = zero_row
    for a in range(steps):
        for b in range(a, steps):
            product = past_sets[a, 0] * past_sets[b, 0]
            for t in range(1, count):
                product = product + past_sets[a, t] * past_sets[b, t]
            value = jnp.sum(jnp.sum(product, axis=0, keepdims=True), axis=1, keepdims=True)
            pair_lane[(a, b)] = len(pair_lane)
            gram = jnp.where(lane == pair_lane[(a, b)], value, gram)

    row = lax.broadcasted_iota(jnp.int32, (ROWS, slots), 0)
    wide_row = lax.broadcasted_iota(jnp.int32, (ROWS, 2 * slots), 0)

    square_row = lax.broadcasted_iota(jnp.int32, (slots, slots), 0)
    square_lane = lax.broadcasted_iota(jnp.int32, (slots, slots), 1)

    def flat_of(place):
        return (place[0] * wraps[1] + place[1]) * wraps[2] + place[2]

    def wrap(value, size):
        return jnp.where(value < 0, value + size, value)

    def prepare(place):
        flat = flat_of(place)
        tile = geom[place[0], place[1], place[2]]
        moved = []
        for axis in range(3):
            number = jnp.where(place[axis] == wraps[axis] - 1, -1, place[axis])
            moved.append(CELL_EDGE * (number.astype(jnp.float32) - 0.5 * tiles[axis]))
        offset = jnp.where(row < 2, moved[0], jnp.where(row < 4, moved[1], jnp.where(row < 6, moved[2], 0.0)))
        tile = tile + offset
        spots[flat] = tile
        upright = tile.T
        for c in range(4):
            columns[flat, c] = jnp.broadcast_to(upright[:, 2 * c : 2 * c + 1], (slots, slots))

    def split(t):
        return lax.shift_right_logical(t, 1), lax.bitwise_and(t, 1)

    def pair_weights(t, along, itself):
        first_y, first_z = split(t)
        base = (jnp.int32(0), first_y, first_z)
        place = tuple(wrap(base[i] + along[i], wraps[i]) for i in range(3))
        k = 9 * (along[0] + 1) + 3 * (along[1] + 1) + along[2] + 1
        source = flat_of(place)
        own = flat_of(base)
        here = [spots[own, pl.ds(2 * c, 1), :] for c in range(4)]
        allowed = mask_ref[0, first_y, first_z, k].astype(jnp.float32)
        damp = here[3] * (-THOLE_DAMP * allowed)
        for first in range(0, slots, BLOCK):
            part = pl.ds(first, BLOCK)
            dx = columns[source, 0, part, :] - here[0]
            dy = columns[source, 1, part, :] - here[1]
            dz = columns[source, 2, part, :] - here[2]
            square = dx * dx + dy * dy + (dz * dz + SOFTENING)
            root = lax.rsqrt(square)
            root_two = root * root
            cube = root_two * root
            arg = (square * square) * root * (damp * columns[source, 3, part, :])
            fade = jnp.exp2(arg * LOG2E)
            three = 1.0 - fade
            five = three + arg * fade
            radial, direct = five * cube * root_two, three * cube
            if itself:
                apart = square_row[first : first + BLOCK] != square_lane[first : first + BLOCK]
                radial, direct = jnp.where(apart, radial, 0.0), jnp.where(apart, direct, 0.0)
            both = jnp.concatenate([radial, direct], axis=1)
            high = both.astype(jnp.bfloat16)
            weights[t, k, part, :] = high
            weights[t, k, pl.ds(slots + first, BLOCK), :] = (both - high.astype(jnp.float32)).astype(jnp.bfloat16)

    def outward(t):
        first_y, first_z = split(t)
        return 2 * first_y - 1, 2 * first_z - 1

    def inner_pairs(t, carry):
        out_y, out_z = outward(t)
        for q in range(4):
            pair_weights(t, (0, -out_y * (q // 2), -out_z * (q % 2)), q == 0)
        return carry

    def edge_pairs(t, carry):
        out_y, out_z = outward(t)
        for along in ((out_y, -1), (out_y, 0), (out_y, 1), (0, out_z), (-out_y, out_z)):
            pair_weights(t, (0,) + along, False)
        return carry

    def plane_pairs(along_x):
        def one(t, carry):
            for q in range(9):
                pair_weights(t, (along_x, q // 3 - 1, q % 3 - 1), False)
            return carry

        return one

    for place in places:
        prepare(tuple(jnp.int32(part) for part in place))
    lax.fori_loop(0, count, inner_pairs, 0)

    pl.semaphore_wait(barrier, len(greeted))
    share(0, 0, slots_a, gram)
    geom_copies = halo(geom, send_geom, recv_geom)
    for copy in geom_copies:
        copy.start()
    past_copies = halo(held_past, send_past, recv_past)
    for copy in past_copies:
        copy.start()
    for copy in geom_copies:
        copy.wait()

    for y in range(wraps[1]):
        for z in range(wraps[2]):
            if y >= tiles[1] or z >= tiles[2]:
                prepare((jnp.int32(0), jnp.int32(y), jnp.int32(z)))

    def prepare_eight(step, carry):
        half_x, half_y = split(step)
        for q in range(8):
            prepare((1 + half_x, 2 * half_y + q // 4, jnp.int32(q % 4)))
        return carry

    lax.fori_loop(0, 4, prepare_eight, 0)
    share(0, 1, slots_b, collect(0, 0, slots_a))
    lax.fori_loop(0, count, edge_pairs, 0)
    lax.fori_loop(0, count, plane_pairs(-1), 0)
    lax.fori_loop(0, count, plane_pairs(1), 0)

    def cycle(value):
        value = value + pltpu.roll(value, 4, 0)
        return value + pltpu.roll(value, 2, 0)

    def rounded(value):
        return value.astype(jnp.bfloat16).astype(jnp.float32)

    def set_features(pair, moment):
        twice = [2 * pair, 2 * pair + 1]
        spot = jnp.concatenate([spots[flat] for flat in twice], axis=1)
        spot = jnp.where(wide_row < rows, spot, 0.0)
        by = [
            jnp.concatenate([spots[flat, pl.ds(2 * c, 1), :] for flat in twice], axis=1) * moment
            for c in range(3)
        ]
        first = jnp.concatenate([moment, by[0]], axis=0)
        second = jnp.concatenate(by[1:], axis=0)
        third = cycle(spot * moment) * spot
        middle = third - rounded(third)
        last = middle - rounded(middle)
        blocks = []
        for piece in range(3):
            blocks += [first, second]
            if piece < 2:
                first = first - rounded(first)
                second = second - rounded(second)
        blocks.append(jnp.concatenate([third, middle], axis=0))
        blocks.append(jnp.concatenate([last, jnp.zeros_like(last)], axis=0))
        for number, value in enumerate(blocks):
            features[pair, pl.ds(2 * ROWS * number, 2 * ROWS), :] = value.astype(jnp.bfloat16)

    def along_of(k):
        return (k // 9 - 1, k // 3 % 3 - 1, k % 3 - 1)

    def target_of(place, k):
        along = along_of(k)
        return tuple((place[i] + along[i] + wraps[i]) % wraps[i] for i in range(3))

    def distance(place):
        return sum(part >= n for part, n in zip(place, tiles))

    def partial_sums(t, chosen):
        acc = None
        for k in range(27):
            place = target_of(places[t], k)
            if distance(place) in chosen:
                flat = flat_of(place)
                side = features[flat // 2, :, pl.ds(flat % 2 * slots, slots)]
                part = jnp.dot(
                    jnp.concatenate([side, side], axis=1), weights[t, k], preferred_element_type=jnp.float32
                )
                acc = part if acc is None else acc + part
        group = [acc[ROWS * g : ROWS * (g + 1)] for g in range(2 * ROWS)]
        sums = [(group[8 + g] + group[4 + g] + group[g])[:, 0:slots] for g in range(4)]
        sums.append((group[14] + group[13] + group[12])[:, 0:slots])
        sums.append((group[8] + group[4] + group[0])[:, slots : 2 * slots])
        return sums

    def field_of(t, sums):
        plain, by_x, by_y, by_z, whole, direct = sums
        spot = jnp.where(row < rows, spots[flat_of(places[t])], 0.0)
        mine = [cycle(spot * value) for value in (by_x, by_y, by_z)]
        middle = jnp.where(row < 2, by_x, jnp.where(row < 4, by_y, by_z))
        drawn = jnp.where(row < 2, mine[0], jnp.where(row < 4, mine[1], mine[2]))
        radial = whole - drawn + spot * cycle(spot * plain - middle)
        return jnp.where(row < rows, 3.0 * radial - direct, 0.0)

    fixed = [
        jnp.concatenate([perm_ref[c, x, y, z, :].reshape(1, slots) for c in order] + [spare], axis=0)
        for (x, y, z) in places
    ]
    for copy in past_copies:
        copy.wait()
    total = collect(0, 1, slots_b)
    coeffs = [jnp.broadcast_to(value, (ROWS, slots)) for value in solve_fit(total, past, lane, pair_lane)]

    def predicted(x, y, z):
        value = coeffs[0] * held_past[x, y, z, pl.ds(0, ROWS), :]
        for h in range(1, past):
            value = value + coeffs[h] * held_past[x, y, z, pl.ds(ROWS * h, ROWS), :]
        return value

    def predict(step, carry):
        x, y = lax.shift_right_logical(step, 2), lax.bitwise_and(step, 3)
        for half in range(2):
            moment = jnp.concatenate([predicted(x, y, 2 * half), predicted(x, y, 2 * half + 1)], axis=1)
            set_features(2 * step + half, moment)
        return carry

    lax.fori_loop(0, wraps[0] * wraps[1], predict, 0)
    ones = []
    for t, (x, y, z) in enumerate(places):
        field = field_of(t, partial_sums(t, (0, 1, 2, 3)))
        value = (1.0 - RELAXATION) * predicted(x, y, z) + scaled[t] * (fixed[t] + field)
        held_two[x, y, z] = value
        ones.append(value)
    two_copies = halo(held_two, send_two, recv_two)
    for copy in two_copies:
        copy.start()
    pairs = [(x, y, z) for x in range(wraps[0]) for y in range(wraps[1]) for z in range(0, wraps[2], 2)]
    sums = [None] * count
    for near_by in ((0,), (1,), (2,), (3,)):
        for move, copy in zip(moves, two_copies):
            if sum(part[0] != 0 for part in move) in near_by:
                copy.wait()
        for x, y, z in pairs:
            if distance((x, y, z)) in near_by:
                set_features(
                    flat_of((x, y, z)) // 2,
                    jnp.concatenate([held_two[x, y, z], held_two[x, y, z + 1]], axis=1),
                )
        for t in range(count):
            found = partial_sums(t, near_by)
            sums[t] = found if sums[t] is None else [a + b for a, b in zip(sums[t], found)]
    field = [field_of(t, sums[t]) for t in range(count)]
    changed = jnp.zeros((ROWS, slots), jnp.float32)
    size = jnp.zeros((ROWS, slots), jnp.float32)
    for t, (x, y, z) in enumerate(places):
        before = ones[t]
        after = (1.0 - RELAXATION) * before + scaled[t] * (fixed[t] + field[t])
        for c in range(rows):
            out_ref[c, x, y, z, :] = after[row_of(c)]
        changed = changed + (after - before) * (after - before)
        size = size + after * after

    def all_of(value):
        return jnp.sum(jnp.sum(value, axis=0, keepdims=True), axis=1, keepdims=True)

    pair = jnp.where(lane == 0, all_of(changed), jnp.where(lane == 1, all_of(size), 0.0))
    share(1, 0, slots_c, pair)
    share(1, 1, slots_d, collect(1, 0, slots_c))
    pair = collect(1, 1, slots_d)
    above = jnp.sum(jnp.where(lane == 0, pair, 0.0), axis=1, keepdims=True)
    below = jnp.sum(jnp.where(lane == 1, pair, 0.0), axis=1, keepdims=True)
    change_ref[...] = jnp.broadcast_to(jnp.sqrt(above / (below + 1.0)), (1, slots))


def solution(mesh):
    devices = tuple(mesh.shape[axis] for axis in AXES)

    def on_device(fractions, polarizability, occupancy, pair_mask, perm_field, history):
        tiles = fractions.shape[1:4]
        slots = fractions.shape[4]
        count = tiles[0] * tiles[1] * tiles[2]
        wraps = tuple(n + 2 for n in tiles)
        total_tiles = wraps[0] * wraps[1] * wraps[2]
        moves = len(halo_moves(tiles))
        past = history.shape[0] - 1
        vmem = pl.BlockSpec(memory_space=pltpu.VMEM)
        f32 = jnp.float32
        groups = [devices[0], devices[1] * devices[2]]
        induced, change = pl.pallas_call(
            functools.partial(kernel, devices),
            out_shape=(
                jax.ShapeDtypeStruct(perm_field.shape, f32),
                jax.ShapeDtypeStruct((1, slots), f32),
            ),
            in_specs=[pl.BlockSpec(memory_space=pltpu.HBM)] * 6,
            out_specs=(vmem, vmem),
            scratch_shapes=[
                pltpu.VMEM(fractions.shape, f32),
                pltpu.VMEM(polarizability.shape, f32),
                pltpu.VMEM(occupancy.shape, jnp.int32),
                pltpu.SMEM(pair_mask.shape, jnp.int32),
                pltpu.VMEM(perm_field.shape, f32),
                pltpu.VMEM(history.shape, f32),
                pltpu.VMEM(wraps + (ROWS, slots), f32),
                pltpu.VMEM(wraps + (past * ROWS, slots), f32),
                pltpu.VMEM(wraps + (ROWS, slots), f32),
                pltpu.VMEM((history.shape[0], count, ROWS, slots), f32),
                pltpu.VMEM((total_tiles, ROWS, slots), f32),
                pltpu.VMEM((total_tiles, 4, slots, slots), f32),
                pltpu.VMEM((total_tiles // 2, 16 * ROWS, 2 * slots), jnp.bfloat16),
                pltpu.VMEM((count, 27, 2 * slots, 2 * slots), jnp.bfloat16),
            ]
            + [pltpu.VMEM((n, 1, slots), f32) for n in groups * 2]
            + [
                pltpu.SemaphoreType.DMA((6,)),
                pltpu.SemaphoreType.DMA((2, 2)),
                pltpu.SemaphoreType.DMA((2, 2)),
            ]
            + [pltpu.SemaphoreType.DMA((moves,))] * 6,
            compiler_params=pltpu.CompilerParams(
                collective_id=0, has_side_effects=True, vmem_limit_bytes=67043328
            ),
        )(fractions, polarizability, occupancy, pair_mask, perm_field, history)
        return induced, change[0, 0]

    in_specs = (
        P(None, "gx", "gy", "gz", None),
        P("gx", "gy", "gz", None),
        P("gx", "gy", "gz", None),
        P("gx", "gy", "gz", None),
        P(None, "gx", "gy", "gz", None),
        P(None, None, "gx", "gy", "gz", None),
    )
    out_specs = (P(None, "gx", "gy", "gz", None), P())
    return jax.shard_map(
        on_device, mesh=mesh, in_specs=in_specs, out_specs=out_specs, check_vma=False
    )
```

time: 73 us -> 57.3 us (0.78)
  Pallas kernels: 69.7 us -> 54 us
    pallas_call x1, Pallas kernels: 69.7 us -> 54 us  [on_device(): pl.pallas_call(functools.partial(kernel, devices), out_shape=(jax.ShapeDt...]
where the time goes in v2:
time: 57.3 us; the launch traced here: 57.1 us
  Pallas kernels  54 us (94%)
  between operations  1.81 us (3%)
  local copies, waits for them, and re-layouts  1.31 us (2%)
    pallas_call x1, Pallas kernels, on_device(): pl.pallas_call(functools.partial(kernel, devices), out_shape=(jax.ShapeDt...  54 us
    unnamed x3, local copies, waits for them, and re-layouts  1.31 us

profile of v2, /device:TPU:1, one launch (start us, length us, event | category | flops | bytes accessed | tf_op | source)
XLA Modules:
  0.0 57.1 jit_solution(3356306872316353835)
XLA Ops:
  0.6 54.0 %shard_map.77 = (f32[6,1,2,2,128]{4,3,2,1,0:T(2,128)}, f32[1,128]{1,0:T(1,128)}) custom-call(f32[3,1,2,2,128]{4,3,2,1,0:T(2,128)} %frac_in.1, f32[1,2,2,128]{3,2,1,0:T(2,128)} %pol_in.1, s32[1,2,2,128]{3,2,1,0:T(2,128)} %occ_in.1, s32[1,2,2,27]{3,2,1,0:T(2,128)} %mask_in.1, f32[6,1,2,2,128]{4,3,2,1,0:T(2,128)} %perm_in.1, f32[6,6,1,2,2,128]{5,4,3,2,1,0:T(2,128)} %hist_in.1), custom_call_target="tpu_custom_call" | custom-call | tf_op jit(solution)/shard_map/pallas_call | solution.py:482
  54.6 0.0 copy-start
  54.6 1.3 %copy.10 = f32[6,1,2,2,128]{4,3,2,1,0:T(2,128)} copy(f32[6,1,2,2,128]{4,3,2,1,0:T(2,128)} %get-tuple-element.8) | data formatting | bytes 24576
  56.0 0.0 copy-done
Async XLA Ops:
  54.6 1.3 %copy-start = (f32[1,128]{1,0:T(1,128)S(1)}, f32[1,128]{1,0:T(1,128)}, u32[]{:S(2)}) copy-start(f32[1,128]{1,0:T(1,128)} %get-tuple-element.5) | copy-start | bytes 1540

commit v3 on v2

--- a/solution.py
+++ b/solution.py
@@ -70,8 +70,8 @@
     out_ref, change_ref,
     frac_ref, pol_ref, occ_ref, mask_ref, perm_ref, hist_ref,
     geom, held_past, held_two, past_sets, spots, columns, features, weights,
-    slots_a, slots_b, slots_c, slots_d,
-    load_sem, send_all, recv_all, send_geom, recv_geom, send_past, recv_past, send_two, recv_two,
+    slots_a, slots_b, slots_c, slots_d, measure,
+    load_sem, send_all, recv_all, send_near, recv_near,
 ):
     tiles = tuple(frac_ref.shape[1:4])
     wraps = tuple(n + 2 for n in tiles)
@@ -82,6 +82,38 @@
     at = [lax.axis_index(axis) for axis in AXES]
     moves = halo_moves(tiles)
     lane = lax.broadcasted_iota(jnp.int32, (1, slots), 1)
+
+    def size_of(axes):
+        total = 1
+        for axis in axes:
+            total *= devices[axis]
+        return total
+
+    def shifted(shift):
+        places = []
+        for axis in range(3):
+            place = at[axis] + shift[axis]
+            places.append(jnp.where(place >= devices[axis], place - devices[axis], place))
+        return tuple(places)
+
+    def hops(shift):
+        return sum(min(part, n - part) for part, n in zip(shift, devices))
+
+    def shifts_of(axes):
+        spans = [range(devices[axis]) if axis in axes else range(1) for axis in range(3)]
+        every = [(x, y, z) for x in spans[0] for y in spans[1] for z in spans[2] if (x, y, z) != (0, 0, 0)]
+        return sorted(every, key=lambda shift: -hops(shift))
+
+    def rank_in(axes):
+        rank = 0
+        for axis in axes:
+            rank = rank * devices[axis] + at[axis]
+        return rank
+
+    near = [tuple((move[axis][0] + devices[axis]) % devices[axis] for axis in range(3)) for move in moves]
+    greeted = list(dict.fromkeys([shift for axes in GROUPS for shift in shifts_of(axes)] + near))
+
+    barrier = pltpu.get_barrier_semaphore()
     loads = [
         pltpu.make_async_copy(source, target, load_sem.at[number])
         for number, (source, target) in enumerate(
@@ -93,38 +125,6 @@
     ]
     for load in loads:
         load.start()
-
-    def size_of(axes):
-        total = 1
-        for axis in axes:
-            total *= devices[axis]
-        return total
-
-    def shifted(shift):
-        places = []
-        for axis in range(3):
-            place = at[axis] + shift[axis]
-            places.append(jnp.where(place >= devices[axis], place - devices[axis], place))
-        return tuple(places)
-
-    def hops(shift):
-        return sum(min(part, n - part) for part, n in zip(shift, devices))
-
-    def shifts_of(axes):
-        spans = [range(devices[axis]) if axis in axes else range(1) for axis in range(3)]
-        every = [(x, y, z) for x in spans[0] for y in spans[1] for z in spans[2] if (x, y, z) != (0, 0, 0)]
-        return sorted(every, key=lambda shift: -hops(shift))
-
-    def rank_in(axes):
-        rank = 0
-        for axis in axes:
-            rank = rank * devices[axis] + at[axis]
-        return rank
-
-    near = [tuple((move[axis][0] + devices[axis]) % devices[axis] for axis in range(3)) for move in moves]
-    greeted = list(dict.fromkeys([shift for axes in GROUPS for shift in shifts_of(axes)] + near))
-
-    barrier = pltpu.get_barrier_semaphore()
 
     for shift in greeted:
         pl.semaphore_signal(barrier, inc=1, device_id=shifted(shift), device_id_type=MESH)
@@ -159,22 +159,36 @@
         whole.wait_recv()
         return jnp.sum(held[...], axis=0)
 
-    def halo(held, send, recv):
-        copies = []
-        for number, move in enumerate(moves):
+    def halo(held, send, recv, crossed):
+        for move, shift in zip(moves, near):
+            if sum(part[0] != 0 for part in move) not in crossed:
+                continue
             source = tuple(pl.ds(part[1], part[2]) for part in move)
             place = tuple(pl.ds(part[3], part[2]) for part in move)
-            copies.append(
-                pltpu.make_async_remote_copy(
-                    src_ref=held.at[source],
-                    dst_ref=held.at[place],
-                    send_sem=send.at[number],
-                    recv_sem=recv.at[number],
-                    device_id=shifted(near[number]),
-                    device_id_type=MESH,
-                )
-            )
-        return copies
+            pltpu.make_async_remote_copy(
+                src_ref=held.at[source],
+                dst_ref=held.at[place],
+                send_sem=send,
+                recv_sem=recv,
+                device_id=shifted(shift),
+                device_id_type=MESH,
+            ).start()
+
+    def halo_wait(held, send, recv, crossed):
+        amount = 0
+        for move in moves:
+            if sum(part[0] != 0 for part in move) in crossed:
+                amount += move[0][2] * move[1][2] * move[2][2] * (held.shape[3] // ROWS)
+        whole = pltpu.make_async_remote_copy(
+            src_ref=measure.at[pl.ds(0, amount)],
+            dst_ref=measure.at[pl.ds(0, amount)],
+            send_sem=send,
+            recv_sem=recv,
+            device_id=shifted(near[0]),
+            device_id_type=MESH,
+        )
+        whole.wait_send()
+        whole.wait_recv()
 
     def row_of(c):
         return 2 * (c % 3) + c // 3
@@ -223,6 +237,19 @@
     def wrap(value, size):
         return jnp.where(value < 0, value + size, value)
 
+    def rounded(value):
+        return value.astype(jnp.bfloat16).astype(jnp.float32)
+
+    piece_row = lax.broadcasted_iota(jnp.int32, (4 * ROWS, 4 * slots), 0)
+    piece_lane = lax.broadcasted_iota(jnp.int32, (4 * ROWS, 4 * slots), 1)
+    chosen_rows = jnp.where(
+        jnp.logical_and(
+            lax.bitwise_and(piece_row, ROWS - 1) == 2 * lax.shift_right_logical(piece_lane, 7), piece_row < 3 * ROWS
+        ),
+        1.0,
+        0.0,
+    ).astype(jnp.bfloat16)
+
     def prepare(place):
         flat = flat_of(place)
         tile = geom[place[0], place[1], place[2]]
@@ -233,9 +260,12 @@
         offset = jnp.where(row < 2, moved[0], jnp.where(row < 4, moved[1], jnp.where(row < 6, moved[2], 0.0)))
         tile = tile + offset
         spots[flat] = tile
-        upright = tile.T
+        middle = tile - rounded(tile)
+        last = middle - rounded(middle)
+        upright = jnp.concatenate([tile, middle, last, jnp.zeros_like(tile)], axis=0).T
+        spread = jnp.dot(upright.astype(jnp.bfloat16), chosen_rows, preferred_element_type=jnp.float32)
         for c in range(4):
-            columns[flat, c] = jnp.broadcast_to(upright[:, 2 * c : 2 * c + 1], (slots, slots))
+            columns[flat, c] = spread[:, c * slots : (c + 1) * slots]
 
     def split(t):
         return lax.shift_right_logical(t, 1), lax.bitwise_and(t, 1)
@@ -302,14 +332,10 @@
 
     pl.semaphore_wait(barrier, len(greeted))
     share(0, 0, slots_a, gram)
-    geom_copies = halo(geom, send_geom, recv_geom)
-    for copy in geom_copies:
-        copy.start()
-    past_copies = halo(held_past, send_past, recv_past)
-    for copy in past_copies:
-        copy.start()
-    for copy in geom_copies:
-        copy.wait()
+    everywhere = (1, 2, 3)
+    halo(geom, send_near.at[0], recv_near.at[0], everywhere)
+    halo(held_past, send_near.at[1], recv_near.at[1], everywhere)
+    halo_wait(geom, send_near.at[0], recv_near.at[0], everywhere)
 
     for y in range(wraps[1]):
         for z in range(wraps[2]):
@@ -331,9 +357,6 @@
     def cycle(value):
         value = value + pltpu.roll(value, 4, 0)
         return value + pltpu.roll(value, 2, 0)
-
-    def rounded(value):
-        return value.astype(jnp.bfloat16).astype(jnp.float32)
 
     def set_features(pair, moment):
         twice = [2 * pair, 2 * pair + 1]
@@ -399,8 +422,7 @@
         jnp.concatenate([perm_ref[c, x, y, z, :].reshape(1, slots) for c in order] + [spare], axis=0)
         for (x, y, z) in places
     ]
-    for copy in past_copies:
-        copy.wait()
+    halo_wait(held_past, send_near.at[1], recv_near.at[1], everywhere)
     total = collect(0, 1, slots_b)
     coeffs = [jnp.broadcast_to(value, (ROWS, slots)) for value in solve_fit(total, past, lane, pair_lane)]
 
@@ -424,15 +446,13 @@
         value = (1.0 - RELAXATION) * predicted(x, y, z) + scaled[t] * (fixed[t] + field)
         held_two[x, y, z] = value
         ones.append(value)
-    two_copies = halo(held_two, send_two, recv_two)
-    for copy in two_copies:
-        copy.start()
+    for crossed in (3, 2, 1):
+        halo(held_two, send_near.at[1 + crossed], recv_near.at[1 + crossed], (crossed,))
     pairs = [(x, y, z) for x in range(wraps[0]) for y in range(wraps[1]) for z in range(0, wraps[2], 2)]
     sums = [None] * count
     for near_by in ((0,), (1,), (2,), (3,)):
-        for move, copy in zip(moves, two_copies):
-            if sum(part[0] != 0 for part in move) in near_by:
-                copy.wait()
+        if near_by != (0,):
+            halo_wait(held_two, send_near.at[1 + near_by[0]], recv_near.at[1 + near_by[0]], near_by)
         for x, y, z in pairs:
             if distance((x, y, z)) in near_by:
                 set_features(
@@ -474,7 +494,6 @@
         count = tiles[0] * tiles[1] * tiles[2]
         wraps = tuple(n + 2 for n in tiles)
         total_tiles = wraps[0] * wraps[1] * wraps[2]
-        moves = len(halo_moves(tiles))
         past = history.shape[0] - 1
         vmem = pl.BlockSpec(memory_space=pltpu.VMEM)
         f32 = jnp.float32
@@ -504,12 +523,13 @@
                 pltpu.VMEM((count, 27, 2 * slots, 2 * slots), jnp.bfloat16),
             ]
             + [pltpu.VMEM((n, 1, slots), f32) for n in groups * 2]
+            + [pltpu.VMEM(((total_tiles - count) * past, ROWS, slots), f32)]
             + [
                 pltpu.SemaphoreType.DMA((6,)),
                 pltpu.SemaphoreType.DMA((2, 2)),
                 pltpu.SemaphoreType.DMA((2, 2)),
             ]
-            + [pltpu.SemaphoreType.DMA((moves,))] * 6,
+            + [pltpu.SemaphoreType.DMA((5,))] * 2,
             compiler_params=pltpu.CompilerParams(
                 collective_id=0, has_side_effects=True, vmem_limit_bytes=67043328
             ),

time: 57.3 us -> 54.1 us (0.944)
  Pallas kernels: 54 us -> 50.8 us
    pallas_call x1, Pallas kernels: 54 us -> 50.8 us  [on_device(): pl.pallas_call(functools.partial(kernel, devices), out_shape=(jax.ShapeDt...]
where the time goes in v3:
time: 54.1 us; the launch traced here: 53.9 us
  Pallas kernels  50.8 us (94%)
  between operations  1.81 us (3%)
  local copies, waits for them, and re-layouts  1.31 us (2%)
    pallas_call x1, Pallas kernels, on_device(): pl.pallas_call(functools.partial(kernel, devices), out_shape=(jax.ShapeDt...  50.8 us
    unnamed x3, local copies, waits for them, and re-layouts  1.31 us

profile of v3, /device:TPU:1, one launch (start us, length us, event | category | flops | bytes accessed | tf_op | source)
XLA Modules:
  0.0 53.9 jit_solution(7582526769707088783)
XLA Ops:
  0.6 50.8 %shard_map.77 = (f32[6,1,2,2,128]{4,3,2,1,0:T(2,128)}, f32[1,128]{1,0:T(1,128)}) custom-call(f32[3,1,2,2,128]{4,3,2,1,0:T(2,128)} %frac_in.1, f32[1,2,2,128]{3,2,1,0:T(2,128)} %pol_in.1, s32[1,2,2,128]{3,2,1,0:T(2,128)} %occ_in.1, s32[1,2,2,27]{3,2,1,0:T(2,128)} %mask_in.1, f32[6,1,2,2,128]{4,3,2,1,0:T(2,128)} %perm_in.1, f32[6,6,1,2,2,128]{5,4,3,2,1,0:T(2,128)} %hist_in.1), custom_call_target="tpu_custom_call" | custom-call | tf_op jit(solution)/shard_map/pallas_call | solution.py:501
  51.4 0.0 copy-start
  51.4 1.3 %copy.10 = f32[6,1,2,2,128]{4,3,2,1,0:T(2,128)} copy(f32[6,1,2,2,128]{4,3,2,1,0:T(2,128)} %get-tuple-element.8) | data formatting | bytes 24576
  52.7 0.0 copy-done
Async XLA Ops:
  51.4 1.3 %copy-start = (f32[1,128]{1,0:T(1,128)S(1)}, f32[1,128]{1,0:T(1,128)}, u32[]{:S(2)}) copy-start(f32[1,128]{1,0:T(1,128)} %get-tuple-element.5) | copy-start | bytes 1540

commit v4 on v3

--- a/solution.py
+++ b/solution.py
@@ -83,37 +83,6 @@
     moves = halo_moves(tiles)
     lane = lax.broadcasted_iota(jnp.int32, (1, slots), 1)
 
-    def size_of(axes):
-        total = 1
-        for axis in axes:
-            total *= devices[axis]
-        return total
-
-    def shifted(shift):
-        places = []
-        for axis in range(3):
-            place = at[axis] + shift[axis]
-            places.append(jnp.where(place >= devices[axis], place - devices[axis], place))
-        return tuple(places)
-
-    def hops(shift):
-        return sum(min(part, n - part) for part, n in zip(shift, devices))
-
-    def shifts_of(axes):
-        spans = [range(devices[axis]) if axis in axes else range(1) for axis in range(3)]
-        every = [(x, y, z) for x in spans[0] for y in spans[1] for z in spans[2] if (x, y, z) != (0, 0, 0)]
-        return sorted(every, key=lambda shift: -hops(shift))
-
-    def rank_in(axes):
-        rank = 0
-        for axis in axes:
-            rank = rank * devices[axis] + at[axis]
-        return rank
-
-    near = [tuple((move[axis][0] + devices[axis]) % devices[axis] for axis in range(3)) for move in moves]
-    greeted = list(dict.fromkeys([shift for axes in GROUPS for shift in shifts_of(axes)] + near))
-
-    barrier = pltpu.get_barrier_semaphore()
     loads = [
         pltpu.make_async_copy(source, target, load_sem.at[number])
         for number, (source, target) in enumerate(
@@ -126,6 +95,37 @@
     for load in loads:
         load.start()
 
+    def size_of(axes):
+        total = 1
+        for axis in axes:
+            total *= devices[axis]
+        return total
+
+    def shifted(shift):
+        places = []
+        for axis in range(3):
+            place = at[axis] + shift[axis]
+            places.append(jnp.where(place >= devices[axis], place - devices[axis], place))
+        return tuple(places)
+
+    def hops(shift):
+        return sum(min(part, n - part) for part, n in zip(shift, devices))
+
+    def shifts_of(axes):
+        spans = [range(devices[axis]) if axis in axes else range(1) for axis in range(3)]
+        every = [(x, y, z) for x in spans[0] for y in spans[1] for z in spans[2] if (x, y, z) != (0, 0, 0)]
+        return sorted(every, key=lambda shift: -hops(shift))
+
+    def rank_in(axes):
+        rank = 0
+        for axis in axes:
+            rank = rank * devices[axis] + at[axis]
+        return rank
+
+    near = [tuple((move[axis][0] + devices[axis]) % devices[axis] for axis in range(3)) for move in moves]
+    greeted = list(dict.fromkeys([shift for axes in GROUPS for shift in shifts_of(axes)] + near))
+
+    barrier = pltpu.get_barrier_semaphore()
     for shift in greeted:
         pl.semaphore_signal(barrier, inc=1, device_id=shifted(shift), device_id_type=MESH)
     for load in loads:
@@ -306,53 +306,46 @@
         first_y, first_z = split(t)
         return 2 * first_y - 1, 2 * first_z - 1
 
-    def inner_pairs(t, carry):
-        out_y, out_z = outward(t)
-        for q in range(4):
-            pair_weights(t, (0, -out_y * (q // 2), -out_z * (q % 2)), q == 0)
-        return carry
-
-    def edge_pairs(t, carry):
-        out_y, out_z = outward(t)
-        for along in ((out_y, -1), (out_y, 0), (out_y, 1), (0, out_z), (-out_y, out_z)):
-            pair_weights(t, (0,) + along, False)
-        return carry
-
-    def plane_pairs(along_x):
+    def weigh(choose):
         def one(t, carry):
-            for q in range(9):
-                pair_weights(t, (along_x, q // 3 - 1, q % 3 - 1), False)
+            for along in choose(*outward(t)):
+                pair_weights(t, along, all(isinstance(part, int) and part == 0 for part in along))
             return carry
 
-        return one
-
-    for place in places:
-        prepare(tuple(jnp.int32(part) for part in place))
-    lax.fori_loop(0, count, inner_pairs, 0)
-
+        lax.fori_loop(0, count, one, 0)
+
+    def distance(place):
+        return sum(part >= n for part, n in zip(place, tiles))
+
+    def prepare_at(crossed):
+        for x in range(wraps[0]):
+            for y in range(wraps[1]):
+                for z in range(wraps[2]):
+                    if distance((x, y, z)) == crossed:
+                        prepare((jnp.int32(x), jnp.int32(y), jnp.int32(z)))
+
+    prepare_at(0)
     pl.semaphore_wait(barrier, len(greeted))
     share(0, 0, slots_a, gram)
+    for crossed in (1, 2, 3):
+        halo(geom, send_near.at[crossed - 1], recv_near.at[crossed - 1], (crossed,))
     everywhere = (1, 2, 3)
-    halo(geom, send_near.at[0], recv_near.at[0], everywhere)
-    halo(held_past, send_near.at[1], recv_near.at[1], everywhere)
-    halo_wait(geom, send_near.at[0], recv_near.at[0], everywhere)
-
-    for y in range(wraps[1]):
-        for z in range(wraps[2]):
-            if y >= tiles[1] or z >= tiles[2]:
-                prepare((jnp.int32(0), jnp.int32(y), jnp.int32(z)))
-
-    def prepare_eight(step, carry):
-        half_x, half_y = split(step)
-        for q in range(8):
-            prepare((1 + half_x, 2 * half_y + q // 4, jnp.int32(q % 4)))
-        return carry
-
-    lax.fori_loop(0, 4, prepare_eight, 0)
+    halo(held_past, send_near.at[3], recv_near.at[3], everywhere)
+    weigh(lambda y, z: ((0, 0, 0), (0, 0, -z), (0, -y, 0), (0, -y, -z)))
+    halo_wait(geom, send_near.at[0], recv_near.at[0], (1,))
+    prepare_at(1)
+    weigh(lambda y, z: tuple((-1, -y * b, -z * c) for b in (0, 1) for c in (0, 1)) + ((0, y, 0), (0, y, -z)))
     share(0, 1, slots_b, collect(0, 0, slots_a))
-    lax.fori_loop(0, count, edge_pairs, 0)
-    lax.fori_loop(0, count, plane_pairs(-1), 0)
-    lax.fori_loop(0, count, plane_pairs(1), 0)
+    weigh(lambda y, z: tuple((1, -y * b, -z * c) for b in (0, 1) for c in (0, 1)) + ((0, 0, z), (0, -y, z)))
+    halo_wait(geom, send_near.at[1], recv_near.at[1], (2,))
+    prepare_at(2)
+    weigh(
+        lambda y, z: tuple((x,) + side for x in (-1, 1) for side in ((y, 0), (y, -z), (0, z), (-y, z)))
+        + ((0, y, z),)
+    )
+    halo_wait(geom, send_near.at[2], recv_near.at[2], (3,))
+    prepare_at(3)
+    weigh(lambda y, z: ((-1, y, z), (1, y, z)))
 
     def cycle(value):
         value = value + pltpu.roll(value, 4, 0)
@@ -389,9 +382,6 @@
         along = along_of(k)
         return tuple((place[i] + along[i] + wraps[i]) % wraps[i] for i in range(3))
 
-    def distance(place):
-        return sum(part >= n for part, n in zip(place, tiles))
-
     def partial_sums(t, chosen):
         acc = None
         for k in range(27):
@@ -422,7 +412,7 @@
         jnp.concatenate([perm_ref[c, x, y, z, :].reshape(1, slots) for c in order] + [spare], axis=0)
         for (x, y, z) in places
     ]
-    halo_wait(held_past, send_near.at[1], recv_near.at[1], everywhere)
+    halo_wait(held_past, send_near.at[3], recv_near.at[3], everywhere)
     total = collect(0, 1, slots_b)
     coeffs = [jnp.broadcast_to(value, (ROWS, slots)) for value in solve_fit(total, past, lane, pair_lane)]
 
@@ -432,14 +422,11 @@
             value = value + coeffs[h] * held_past[x, y, z, pl.ds(ROWS * h, ROWS), :]
         return value
 
-    def predict(step, carry):
-        x, y = lax.shift_right_logical(step, 2), lax.bitwise_and(step, 3)
-        for half in range(2):
-            moment = jnp.concatenate([predicted(x, y, 2 * half), predicted(x, y, 2 * half + 1)], axis=1)
-            set_features(2 * step + half, moment)
-        return carry
-
-    lax.fori_loop(0, wraps[0] * wraps[1], predict, 0)
+    pairs = [(x, y, z) for x in range(wraps[0]) for y in range(wraps[1]) for z in range(0, wraps[2], 2)]
+    for x, y, z in pairs:
+        set_features(
+            flat_of((x, y, z)) // 2, jnp.concatenate([predicted(x, y, z), predicted(x, y, z + 1)], axis=1)
+        )
     ones = []
     for t, (x, y, z) in enumerate(places):
         field = field_of(t, partial_sums(t, (0, 1, 2, 3)))
@@ -447,12 +434,11 @@
         held_two[x, y, z] = value
         ones.append(value)
     for crossed in (3, 2, 1):
-        halo(held_two, send_near.at[1 + crossed], recv_near.at[1 + crossed], (crossed,))
-    pairs = [(x, y, z) for x in range(wraps[0]) for y in range(wraps[1]) for z in range(0, wraps[2], 2)]
+        halo(held_two, send_near.at[3 + crossed], recv_near.at[3 + crossed], (crossed,))
     sums = [None] * count
     for near_by in ((0,), (1,), (2,), (3,)):
         if near_by != (0,):
-            halo_wait(held_two, send_near.at[1 + near_by[0]], recv_near.at[1 + near_by[0]], near_by)
+            halo_wait(held_two, send_near.at[3 + near_by[0]], recv_near.at[3 + near_by[0]], near_by)
         for x, y, z in pairs:
             if distance((x, y, z)) in near_by:
                 set_features(
@@ -529,7 +515,7 @@
                 pltpu.SemaphoreType.DMA((2, 2)),
                 pltpu.SemaphoreType.DMA((2, 2)),
             ]
-            + [pltpu.SemaphoreType.DMA((5,))] * 2,
+            + [pltpu.SemaphoreType.DMA((7,))] * 2,
             compiler_params=pltpu.CompilerParams(
                 collective_id=0, has_side_effects=True, vmem_limit_bytes=67043328
             ),

time: 54.1 us -> 51.9 us (0.959)
  Pallas kernels: 50.8 us -> 48.6 us
    pallas_call x1, Pallas kernels: 50.8 us -> 48.6 us  [on_device(): pl.pallas_call(functools.partial(kernel, devices), out_shape=(jax.ShapeDt...]
where the time goes in v4:
time: 51.9 us; the launch traced here: 51.7 us
  Pallas kernels  48.6 us (94%)
  between operations  1.81 us (3%)
  local copies, waits for them, and re-layouts  1.31 us (3%)
    pallas_call x1, Pallas kernels, on_device(): pl.pallas_call(functools.partial(kernel, devices), out_shape=(jax.ShapeDt...  48.6 us
    unnamed x3, local copies, waits for them, and re-layouts  1.31 us

profile of v4, /device:TPU:1, one launch (start us, length us, event | category | flops | bytes accessed | tf_op | source)
XLA Modules:
  0.0 51.7 jit_solution(14776547172603023589)
XLA Ops:
  0.6 48.6 %shard_map.77 = (f32[6,1,2,2,128]{4,3,2,1,0:T(2,128)}, f32[1,128]{1,0:T(1,128)}) custom-call(f32[3,1,2,2,128]{4,3,2,1,0:T(2,128)} %frac_in.1, f32[1,2,2,128]{3,2,1,0:T(2,128)} %pol_in.1, s32[1,2,2,128]{3,2,1,0:T(2,128)} %occ_in.1, s32[1,2,2,27]{3,2,1,0:T(2,128)} %mask_in.1, f32[6,1,2,2,128]{4,3,2,1,0:T(2,128)} %perm_in.1, f32[6,6,1,2,2,128]{5,4,3,2,1,0:T(2,128)} %hist_in.1), custom_call_target="tpu_custom_call" | custom-call | tf_op jit(solution)/shard_map/pallas_call | solution.py:487
  49.2 0.0 copy-start
  49.2 1.3 %copy.10 = f32[6,1,2,2,128]{4,3,2,1,0:T(2,128)} copy(f32[6,1,2,2,128]{4,3,2,1,0:T(2,128)} %get-tuple-element.8) | data formatting | bytes 24576
  50.5 0.0 copy-done
Async XLA Ops:
  49.2 1.3 %copy-start = (f32[1,128]{1,0:T(1,128)S(1)}, f32[1,128]{1,0:T(1,128)}, u32[]{:S(2)}) copy-start(f32[1,128]{1,0:T(1,128)} %get-tuple-element.5) | copy-start | bytes 1540

commit v5 on v4

--- a/solution.py
+++ b/solution.py
@@ -123,7 +123,10 @@
         return rank
 
     near = [tuple((move[axis][0] + devices[axis]) % devices[axis] for axis in range(3)) for move in moves]
-    greeted = list(dict.fromkeys([shift for axes in GROUPS for shift in shifts_of(axes)] + near))
+    greeted = sorted(
+        dict.fromkeys([shift for axes in GROUPS for shift in shifts_of(axes)] + near), key=lambda shift: -hops(shift)
+    )
+    inward = 1 - 2 * lax.bitwise_and(at[0], 1)
 
     barrier = pltpu.get_barrier_semaphore()
     for shift in greeted:
@@ -159,31 +162,38 @@
         whole.wait_recv()
         return jnp.sum(held[...], axis=0)
 
-    def halo(held, send, recv, crossed):
+    def halo(held, send, recv, crossed, on_chip=None):
         for move, shift in zip(moves, near):
             if sum(part[0] != 0 for part in move) not in crossed:
                 continue
+            number = 0
+            if on_chip is not None and move[0][0] != 0:
+                number = jnp.where(inward == move[0][0], on_chip, 0)
             source = tuple(pl.ds(part[1], part[2]) for part in move)
             place = tuple(pl.ds(part[3], part[2]) for part in move)
             pltpu.make_async_remote_copy(
                 src_ref=held.at[source],
                 dst_ref=held.at[place],
-                send_sem=send,
-                recv_sem=recv,
+                send_sem=send.at[number],
+                recv_sem=recv.at[number],
                 device_id=shifted(shift),
                 device_id_type=MESH,
             ).start()
 
-    def halo_wait(held, send, recv, crossed):
-        amount = 0
-        for move in moves:
-            if sum(part[0] != 0 for part in move) in crossed:
-                amount += move[0][2] * move[1][2] * move[2][2] * (held.shape[3] // ROWS)
+    def tiles_of(crossed):
+        return sum(
+            move[0][2] * move[1][2] * move[2][2]
+            for move in moves
+            if sum(part[0] != 0 for part in move) in crossed
+        )
+
+    def halo_wait(held, number, arriving):
+        amount = arriving * (held.shape[3] // ROWS)
         whole = pltpu.make_async_remote_copy(
             src_ref=measure.at[pl.ds(0, amount)],
             dst_ref=measure.at[pl.ds(0, amount)],
-            send_sem=send,
-            recv_sem=recv,
+            send_sem=send_near.at[number],
+            recv_sem=recv_near.at[number],
             device_id=shifted(near[0]),
             device_id_type=MESH,
         )
@@ -317,33 +327,51 @@
     def distance(place):
         return sum(part >= n for part, n in zip(place, tiles))
 
-    def prepare_at(crossed):
-        for x in range(wraps[0]):
+    def prepare_at(crossed, along_x=(0, 1, 2)):
+        for x in along_x:
             for y in range(wraps[1]):
                 for z in range(wraps[2]):
                     if distance((x, y, z)) == crossed:
                         prepare((jnp.int32(x), jnp.int32(y), jnp.int32(z)))
 
+    def prepare_side(side):
+        x = jnp.where(side < 0, wraps[0] - 1, tiles[0])
+        for y in range(tiles[1]):
+            for z in range(tiles[2]):
+                prepare((x, jnp.int32(y), jnp.int32(z)))
+
+    def across(side, y, z):
+        return tuple((side, -y * b, -z * c) for b in (0, 1) for c in (0, 1))
+
     prepare_at(0)
     pl.semaphore_wait(barrier, len(greeted))
     share(0, 0, slots_a, gram)
-    for crossed in (1, 2, 3):
-        halo(geom, send_near.at[crossed - 1], recv_near.at[crossed - 1], (crossed,))
+    def from_sem(first):
+        return send_near.at[pl.ds(first, 8 - first)], recv_near.at[pl.ds(first, 8 - first)]
+
+    halo(geom, *from_sem(0), (1,), on_chip=7)
+    halo(geom, *from_sem(1), (2,))
+    halo(geom, *from_sem(2), (3,))
     everywhere = (1, 2, 3)
-    halo(held_past, send_near.at[3], recv_near.at[3], everywhere)
+    halo(held_past, *from_sem(3), everywhere)
     weigh(lambda y, z: ((0, 0, 0), (0, 0, -z), (0, -y, 0), (0, -y, -z)))
-    halo_wait(geom, send_near.at[0], recv_near.at[0], (1,))
-    prepare_at(1)
-    weigh(lambda y, z: tuple((-1, -y * b, -z * c) for b in (0, 1) for c in (0, 1)) + ((0, y, 0), (0, y, -z)))
+    on_chip_tiles = tiles[1] * tiles[2]
+    halo_wait(geom, 7, on_chip_tiles)
+    prepare_side(inward)
+    weigh(lambda y, z: across(inward, y, z))
+    halo_wait(geom, 0, tiles_of((1,)) - on_chip_tiles)
+    prepare_side(-inward)
+    prepare_at(1, (0,))
+    weigh(lambda y, z: ((0, y, 0), (0, y, -z), (0, 0, z), (0, -y, z)))
     share(0, 1, slots_b, collect(0, 0, slots_a))
-    weigh(lambda y, z: tuple((1, -y * b, -z * c) for b in (0, 1) for c in (0, 1)) + ((0, 0, z), (0, -y, z)))
-    halo_wait(geom, send_near.at[1], recv_near.at[1], (2,))
+    weigh(lambda y, z: across(-inward, y, z))
+    halo_wait(geom, 1, tiles_of((2,)))
     prepare_at(2)
     weigh(
         lambda y, z: tuple((x,) + side for x in (-1, 1) for side in ((y, 0), (y, -z), (0, z), (-y, z)))
         + ((0, y, z),)
     )
-    halo_wait(geom, send_near.at[2], recv_near.at[2], (3,))
+    halo_wait(geom, 2, tiles_of((3,)))
     prepare_at(3)
     weigh(lambda y, z: ((-1, y, z), (1, y, z)))
 
@@ -412,7 +440,7 @@
         jnp.concatenate([perm_ref[c, x, y, z, :].reshape(1, slots) for c in order] + [spare], axis=0)
         for (x, y, z) in places
     ]
-    halo_wait(held_past, send_near.at[3], recv_near.at[3], everywhere)
+    halo_wait(held_past, 3, tiles_of(everywhere))
     total = collect(0, 1, slots_b)
     coeffs = [jnp.broadcast_to(value, (ROWS, slots)) for value in solve_fit(total, past, lane, pair_lane)]
 
@@ -434,11 +462,11 @@
         held_two[x, y, z] = value
         ones.append(value)
     for crossed in (3, 2, 1):
-        halo(held_two, send_near.at[3 + crossed], recv_near.at[3 + crossed], (crossed,))
+        halo(held_two, *from_sem(3 + crossed), (crossed,))
     sums = [None] * count
     for near_by in ((0,), (1,), (2,), (3,)):
         if near_by != (0,):
-            halo_wait(held_two, send_near.at[3 + near_by[0]], recv_near.at[3 + near_by[0]], near_by)
+            halo_wait(held_two, 3 + near_by[0], tiles_of(near_by))
         for x, y, z in pairs:
             if distance((x, y, z)) in near_by:
                 set_features(
@@ -515,7 +543,7 @@
                 pltpu.SemaphoreType.DMA((2, 2)),
                 pltpu.SemaphoreType.DMA((2, 2)),
             ]
-            + [pltpu.SemaphoreType.DMA((7,))] * 2,
+            + [pltpu.SemaphoreType.DMA((8,))] * 2,
             compiler_params=pltpu.CompilerParams(
                 collective_id=0, has_side_effects=True, vmem_limit_bytes=67043328
             ),

time: 51.9 us -> 50.6 us (0.975)
  Pallas kernels: 48.6 us -> 47.3 us
    pallas_call x1, Pallas kernels: 48.6 us -> 47.3 us  [on_device(): pl.pallas_call(functools.partial(kernel, devices), out_shape=(jax.ShapeDt...]
where the time goes in v5:
time: 50.6 us; the launch traced here: 50.4 us
  Pallas kernels  47.3 us (93%)
  between operations  1.81 us (4%)
  local copies, waits for them, and re-layouts  1.31 us (3%)
    pallas_call x1, Pallas kernels, on_device(): pl.pallas_call(functools.partial(kernel, devices), out_shape=(jax.ShapeDt...  47.3 us
    unnamed x3, local copies, waits for them, and re-layouts  1.31 us

profile of v5, /device:TPU:1, one launch (start us, length us, event | category | flops | bytes accessed | tf_op | source)
XLA Modules:
  0.0 50.4 jit_solution(6088786992933293509)
XLA Ops:
  0.6 47.3 %shard_map.77 = (f32[6,1,2,2,128]{4,3,2,1,0:T(2,128)}, f32[1,128]{1,0:T(1,128)}) custom-call(f32[3,1,2,2,128]{4,3,2,1,0:T(2,128)} %frac_in.1, f32[1,2,2,128]{3,2,1,0:T(2,128)} %pol_in.1, s32[1,2,2,128]{3,2,1,0:T(2,128)} %occ_in.1, s32[1,2,2,27]{3,2,1,0:T(2,128)} %mask_in.1, f32[6,1,2,2,128]{4,3,2,1,0:T(2,128)} %perm_in.1, f32[6,6,1,2,2,128]{5,4,3,2,1,0:T(2,128)} %hist_in.1), custom_call_target="tpu_custom_call" | custom-call | tf_op jit(solution)/shard_map/pallas_call | solution.py:515
  47.9 0.0 copy-start
  47.9 1.3 %copy.10 = f32[6,1,2,2,128]{4,3,2,1,0:T(2,128)} copy(f32[6,1,2,2,128]{4,3,2,1,0:T(2,128)} %get-tuple-element.8) | data formatting | bytes 24576
  49.2 0.0 copy-done
Async XLA Ops:
  47.9 1.3 %copy-start = (f32[1,128]{1,0:T(1,128)S(1)}, f32[1,128]{1,0:T(1,128)}, u32[]{:S(2)}) copy-start(f32[1,128]{1,0:T(1,128)} %get-tuple-element.5) | copy-start | bytes 1540

commit v6 on v5

--- a/solution.py
+++ b/solution.py
@@ -162,7 +162,7 @@
         whole.wait_recv()
         return jnp.sum(held[...], axis=0)
 
-    def halo(held, send, recv, crossed, on_chip=None):
+    def halo(held, send, recv, crossed, on_chip=None, sent_rows=None):
         for move, shift in zip(moves, near):
             if sum(part[0] != 0 for part in move) not in crossed:
                 continue
@@ -171,6 +171,8 @@
                 number = jnp.where(inward == move[0][0], on_chip, 0)
             source = tuple(pl.ds(part[1], part[2]) for part in move)
             place = tuple(pl.ds(part[3], part[2]) for part in move)
+            if sent_rows is not None:
+                source, place = source + (pl.ds(0, sent_rows),), place + (pl.ds(0, sent_rows),)
             pltpu.make_async_remote_copy(
                 src_ref=held.at[source],
                 dst_ref=held.at[place],
@@ -187,8 +189,8 @@
             if sum(part[0] != 0 for part in move) in crossed
         )
 
-    def halo_wait(held, number, arriving):
-        amount = arriving * (held.shape[3] // ROWS)
+    def halo_wait(sent_rows, number, arriving):
+        amount = arriving * sent_rows // ROWS
         whole = pltpu.make_async_remote_copy(
             src_ref=measure.at[pl.ds(0, amount)],
             dst_ref=measure.at[pl.ds(0, amount)],
@@ -223,7 +225,8 @@
             ) * full
             past_sets[h, t] = moment
             if h > 0:
-                held_past[x, y, z, pl.ds(ROWS * (h - 1), ROWS), :] = moment
+                held_past[x, y, z, pl.ds(rows * (h - 1), rows), :] = moment[0:rows]
+        held_past[x, y, z, pl.ds(rows * past, ROWS - rows), :] = spare
     pair_lane = {}
     gram = zero_row
     for a in range(steps):
@@ -356,22 +359,22 @@
     halo(held_past, *from_sem(3), everywhere)
     weigh(lambda y, z: ((0, 0, 0), (0, 0, -z), (0, -y, 0), (0, -y, -z)))
     on_chip_tiles = tiles[1] * tiles[2]
-    halo_wait(geom, 7, on_chip_tiles)
+    halo_wait(ROWS, 7, on_chip_tiles)
     prepare_side(inward)
     weigh(lambda y, z: across(inward, y, z))
-    halo_wait(geom, 0, tiles_of((1,)) - on_chip_tiles)
+    halo_wait(ROWS, 0, tiles_of((1,)) - on_chip_tiles)
     prepare_side(-inward)
     prepare_at(1, (0,))
     weigh(lambda y, z: ((0, y, 0), (0, y, -z), (0, 0, z), (0, -y, z)))
     share(0, 1, slots_b, collect(0, 0, slots_a))
     weigh(lambda y, z: across(-inward, y, z))
-    halo_wait(geom, 1, tiles_of((2,)))
+    halo_wait(ROWS, 1, tiles_of((2,)))
     prepare_at(2)
     weigh(
         lambda y, z: tuple((x,) + side for x in (-1, 1) for side in ((y, 0), (y, -z), (0, z), (-y, z)))
         + ((0, y, z),)
     )
-    halo_wait(geom, 2, tiles_of((3,)))
+    halo_wait(ROWS, 2, tiles_of((3,)))
     prepare_at(3)
     weigh(lambda y, z: ((-1, y, z), (1, y, z)))
 
@@ -440,15 +443,15 @@
         jnp.concatenate([perm_ref[c, x, y, z, :].reshape(1, slots) for c in order] + [spare], axis=0)
         for (x, y, z) in places
     ]
-    halo_wait(held_past, 3, tiles_of(everywhere))
+    halo_wait(4 * ROWS, 3, tiles_of(everywhere))
     total = collect(0, 1, slots_b)
     coeffs = [jnp.broadcast_to(value, (ROWS, slots)) for value in solve_fit(total, past, lane, pair_lane)]
 
     def predicted(x, y, z):
         value = coeffs[0] * held_past[x, y, z, pl.ds(0, ROWS), :]
         for h in range(1, past):
-            value = value + coeffs[h] * held_past[x, y, z, pl.ds(ROWS * h, ROWS), :]
-        return value
+            value = value + coeffs[h] * held_past[x, y, z, pl.ds(rows * h, ROWS), :]
+        return jnp.where(row < rows, value, 0.0)
 
     pairs = [(x, y, z) for x in range(wraps[0]) for y in range(wraps[1]) for z in range(0, wraps[2], 2)]
     for x, y, z in pairs:
@@ -462,16 +465,20 @@
         held_two[x, y, z] = value
         ones.append(value)
     for crossed in (3, 2, 1):
-        halo(held_two, *from_sem(3 + crossed), (crossed,))
+        halo(held_two, *from_sem(3 + crossed), (crossed,), sent_rows=rows)
     sums = [None] * count
     for near_by in ((0,), (1,), (2,), (3,)):
         if near_by != (0,):
-            halo_wait(held_two, 3 + near_by[0], tiles_of(near_by))
+            halo_wait(rows, 3 + near_by[0], tiles_of(near_by))
         for x, y, z in pairs:
             if distance((x, y, z)) in near_by:
                 set_features(
                     flat_of((x, y, z)) // 2,
-                    jnp.concatenate([held_two[x, y, z], held_two[x, y, z + 1]], axis=1),
+                    jnp.where(
+                        wide_row < rows,
+                        jnp.concatenate([held_two[x, y, z], held_two[x, y, z + 1]], axis=1),
+                        0.0,
+                    ),
                 )
         for t in range(count):
             found = partial_sums(t, near_by)
@@ -528,7 +535,7 @@
                 pltpu.VMEM(perm_field.shape, f32),
                 pltpu.VMEM(history.shape, f32),
                 pltpu.VMEM(wraps + (ROWS, slots), f32),
-                pltpu.VMEM(wraps + (past * ROWS, slots), f32),
+                pltpu.VMEM(wraps + (4 * ROWS, slots), f32),
                 pltpu.VMEM(wraps + (ROWS, slots), f32),
                 pltpu.VMEM((history.shape[0], count, ROWS, slots), f32),
                 pltpu.VMEM((total_tiles, ROWS, slots), f32),

time: 50.6 us -> 50.3 us (level)
  no operation moved by 1% of the time
where the time goes in v6:
time: 50.3 us; the launch traced here: 50.1 us
  Pallas kernels  47 us (93%)
  between operations  1.81 us (4%)
  local copies, waits for them, and re-layouts  1.31 us (3%)
    pallas_call x1, Pallas kernels, on_device(): pl.pallas_call(functools.partial(kernel, devices), out_shape=(jax.ShapeDt...  47 us
    unnamed x3, local copies, waits for them, and re-layouts  1.31 us

profile of v6, /device:TPU:1, one launch (start us, length us, event | category | flops | bytes accessed | tf_op | source)
XLA Modules:
  0.0 50.1 jit_solution(12747346052891090467)
XLA Ops:
  0.6 47.0 %shard_map.77 = (f32[6,1,2,2,128]{4,3,2,1,0:T(2,128)}, f32[1,128]{1,0:T(1,128)}) custom-call(f32[3,1,2,2,128]{4,3,2,1,0:T(2,128)} %frac_in.1, f32[1,2,2,128]{3,2,1,0:T(2,128)} %pol_in.1, s32[1,2,2,128]{3,2,1,0:T(2,128)} %occ_in.1, s32[1,2,2,27]{3,2,1,0:T(2,128)} %mask_in.1, f32[6,1,2,2,128]{4,3,2,1,0:T(2,128)} %perm_in.1, f32[6,6,1,2,2,128]{5,4,3,2,1,0:T(2,128)} %hist_in.1), custom_call_target="tpu_custom_call" | custom-call | tf_op jit(solution)/shard_map/pallas_call | solution.py:522
  47.6 0.0 copy-start
  47.6 1.3 %copy.10 = f32[6,1,2,2,128]{4,3,2,1,0:T(2,128)} copy(f32[6,1,2,2,128]{4,3,2,1,0:T(2,128)} %get-tuple-element.8) | data formatting | bytes 24576
  48.9 0.0 copy-done
Async XLA Ops:
  47.6 1.3 %copy-start = (f32[1,128]{1,0:T(1,128)S(1)}, f32[1,128]{1,0:T(1,128)}, u32[]{:S(2)}) copy-start(f32[1,128]{1,0:T(1,128)} %get-tuple-element.5) | copy-start | bytes 1540
